TPU v7x, 16 devices: a 4x2x1 block of a 4x4x8 slice. The times are simulated.
16 devices in a mesh: sample: 2 (over y, z), tok: 8 (over x, core).
Axes of the slice: x: 4, y: 2, z: 1, core: 2. Of those that a mesh axis runs over, the one named last changes fastest.
The devices are a block of a 4x4x8 slice.
Arguments:
- s_trunk: bfloat16 [1024, 128], P('tok')
- s_inputs: bfloat16 [1024, 128], P('tok')
- z_trunk: bfloat16 [1024, 1024, 16], P('tok')
- x_noise: float32 [2048, 3], P(('sample', 'tok')), parts along dimension 0
- step_noise: float32 [3, 2048, 3], P(None, ('sample', 'tok')), parts along dimension 1
- sigmas: float32 [4], replicated
- relpos_table: bfloat16 [65, 16], replicated
- w_pair_in: bfloat16 [32, 16], replicated
- w_z_up: bfloat16 [2, 16, 64], replicated
- w_z_down: bfloat16 [2, 32, 16], replicated
- w_pair_bias: bfloat16 [2, 16, 4], replicated
- w_single: bfloat16 [256, 128], replicated
- fourier_w: float32 [256], replicated
- fourier_b: float32 [256], replicated
- w_fourier: bfloat16 [256, 128], replicated
- w_s_up: bfloat16 [2, 128, 512], replicated
- w_s_down: bfloat16 [2, 256, 128], replicated
- w_in: float32 [3, 128], replicated
- w_s_tok: bfloat16 [128, 128], replicated
- w_cond: bfloat16 [2, 128, 768], replicated
- gate_bias: float32 [2, 2, 128], replicated
- w_qkvg: bfloat16 [2, 128, 512], replicated
- w_attn_out: bfloat16 [2, 128, 128], replicated
- w_up: bfloat16 [2, 128, 512], replicated
- w_down: bfloat16 [2, 256, 128], replicated
- w_out: bfloat16 [128, 3], replicated
Outputs:
- output: float32 [2048, 3], P(('sample', 'tok')), parts along dimension 0
There are 2 independent parts. A program takes and returns all parts, laid end to end along the dimension named above; an argument that names none is the same for every part.
All inputs are finite; a program needn't handle non-finite values.
Results may differ from a plain program's by a relative error of at most 0.00403962.
Values are sent between devices in bfloat16 or wider.
A program may use at most 768 MiB of HBM per device.

v0:
```python
import math
import jax
import jax.numpy as jnp
from jax import lax
from jax.sharding import PartitionSpec as P

SIGMA_DATA = 16.0
GAMMA = 0.8
NOISE_SCALE = 1.003
STEP_SCALE = 1.5
MASK_VALUE = -1e9


def layer_norm(values):
    values = values.astype(jnp.float32)
    centered = values - jnp.mean(values, axis=-1, keepdims=True)
    variance = jnp.mean(centered * centered, axis=-1, keepdims=True)
    return centered * lax.rsqrt(variance + 1e-5)


def transition(values, w_up_one, w_down_one):
    hidden = jnp.dot(layer_norm(values).astype(jnp.bfloat16), w_up_one, preferred_element_type=jnp.float32)
    half_width = hidden.shape[-1] // 2
    gated_act = (jax.nn.silu(hidden[..., :half_width]) * hidden[..., half_width:]).astype(jnp.bfloat16)
    return values + jnp.dot(gated_act, w_down_one, preferred_element_type=jnp.float32)


def pair_bias_rows(z_rows, row_start, relpos_table, w_pair_in, w_z_up, w_z_down, w_pair_bias):
    tok_rows = z_rows.shape[0]
    n_tok = z_rows.shape[1]
    c_pair = z_rows.shape[2]
    n_blocks = w_pair_bias.shape[0]
    n_heads = w_pair_bias.shape[2]
    n_bins = relpos_table.shape[0]
    rel_clip = (n_bins - 1) // 2
    row_group = 8
    bias_weight = jnp.transpose(w_pair_bias, (1, 0, 2)).reshape(c_pair, n_blocks * n_heads)
    bin_ids = jnp.arange(n_bins)
    col_ids = jnp.arange(n_tok)

    def one_group(group_idx):
        z_group = lax.dynamic_slice_in_dim(z_rows, group_idx * row_group, row_group, axis=0)
        row_ids = row_start + group_idx * row_group + jnp.arange(row_group)
        bin_index = jnp.clip(row_ids[:, None] - col_ids[None, :] + rel_clip, 0, n_bins - 1)
        one_hot = (bin_index[:, :, None] == bin_ids).astype(jnp.bfloat16)
        rel_feat = jnp.dot(one_hot, relpos_table, preferred_element_type=jnp.float32).astype(jnp.bfloat16)
        pair_in = layer_norm(jnp.concatenate([z_group, rel_feat], axis=-1)).astype(jnp.bfloat16)
        pair_cond = jnp.dot(pair_in, w_pair_in, preferred_element_type=jnp.float32)
        for layer_idx in range(w_z_up.shape[0]):
            pair_cond = transition(pair_cond, w_z_up[layer_idx], w_z_down[layer_idx])
        bias_flat = jnp.dot(layer_norm(pair_cond).astype(jnp.bfloat16), bias_weight, preferred_element_type=jnp.float32)
        return bias_flat.astype(jnp.bfloat16)

    groups = lax.map(one_group, jnp.arange(tok_rows // row_group))
    bias_rows = groups.reshape(tok_rows, n_tok, n_blocks, n_heads)
    return jnp.transpose(bias_rows, (2, 3, 0, 1))


def single_cond(s_base, t_hat, fourier_w, fourier_b, w_fourier, w_s_up, w_s_down):
    noise_level = 0.25 * jnp.log(t_hat / SIGMA_DATA)
    fourier_feat = jnp.cos(2.0 * math.pi * (noise_level * fourier_w + fourier_b))
    single = s_base + jnp.dot(layer_norm(fourier_feat[None, :]).astype(jnp.bfloat16), w_fourier, preferred_element_type=jnp.float32)
    for layer_idx in range(w_s_up.shape[0]):
        single = transition(single, w_s_up[layer_idx], w_s_down[layer_idx])
    return layer_norm(single).astype(jnp.bfloat16)


def solution(mesh):
    part_axes = ("sample", "tok")

    def local_run(s_trunk, s_inputs, z_trunk, x_noise, step_noise, sigmas, relpos_table, w_pair_in, w_z_up, w_z_down, w_pair_bias, w_single, fourier_w, fourier_b, w_fourier, w_s_up, w_s_down, w_in, w_s_tok, w_cond, gate_bias, w_qkvg, w_attn_out, w_up, w_down, w_out):
        tok_rows = z_trunk.shape[0]
        n_tok = z_trunk.shape[1]
        n_valid = n_tok - tok_rows // 4
        n_steps = step_noise.shape[0]
        n_blocks = w_qkvg.shape[0]
        c_token = w_qkvg.shape[1]
        n_heads = w_pair_bias.shape[2]
        head_dim = c_token // n_heads
        score_scale = head_dim ** -0.5
        row_start = lax.axis_index("tok") * tok_rows
        bias_all = pair_bias_rows(z_trunk, row_start, relpos_table, w_pair_in, w_z_up, w_z_down, w_pair_bias)
        key_valid = jnp.arange(n_tok) < n_valid
        joined = layer_norm(jnp.concatenate([s_trunk, s_inputs], axis=-1)).astype(jnp.bfloat16)
        s_base = jnp.dot(joined, w_single, preferred_element_type=jnp.float32)
        x_state = sigmas[0] * x_noise
        for step_idx in range(n_steps):
            sigma_prev = sigmas[step_idx]
            t_hat = sigma_prev * (1.0 + GAMMA)
            x_noisy = x_state + NOISE_SCALE * jnp.sqrt(t_hat * t_hat - sigma_prev * sigma_prev) * step_noise[step_idx]
            single_ln = single_cond(s_base, t_hat, fourier_w, fourier_b, w_fourier, w_s_up, w_s_down)
            noise_var = t_hat * t_hat + SIGMA_DATA * SIGMA_DATA
            r_noisy = x_noisy / jnp.sqrt(noise_var)
            token_acts = jnp.sum(r_noisy[:, :, None] * w_in[None, :, :], axis=1) + jnp.dot(single_ln, w_s_tok, preferred_element_type=jnp.float32)
            for block_idx in range(n_blocks):
                cond_proj = jnp.dot(single_ln, w_cond[block_idx], preferred_element_type=jnp.float32)
                normed = (jax.nn.sigmoid(cond_proj[:, :c_token]) * layer_norm(token_acts) + cond_proj[:, c_token:2 * c_token]).astype(jnp.bfloat16)
                qkvg_proj = jnp.dot(normed, w_qkvg[block_idx], preferred_element_type=jnp.float32)
                query_heads = qkvg_proj[:, :c_token].astype(jnp.bfloat16).reshape(tok_rows, n_heads, head_dim)
                kv_local = qkvg_proj[:, c_token:3 * c_token].astype(jnp.bfloat16)
                kv_all = lax.all_gather(kv_local, "tok", axis=0, tiled=True)
                key_heads = kv_all[:, :c_token].reshape(n_tok, n_heads, head_dim)
                value_heads = kv_all[:, c_token:].reshape(n_tok, n_heads, head_dim)
                scores = jnp.einsum("qhd,khd->hqk", query_heads, key_heads, preferred_element_type=jnp.float32) * score_scale + bias_all[block_idx]
                scores = jnp.where(key_valid, scores, MASK_VALUE)
                attn_probs = jax.nn.softmax(scores, axis=-1).astype(jnp.bfloat16)
                attn_mix = jnp.einsum("hqk,khd->qhd", attn_probs, value_heads, preferred_element_type=jnp.float32).reshape(tok_rows, c_token)
                gated_mix = (jax.nn.sigmoid(qkvg_proj[:, 3 * c_token:]) * attn_mix).astype(jnp.bfloat16)
                attn_out = jnp.dot(gated_mix, w_attn_out[block_idx], preferred_element_type=jnp.float32)
                token_acts = token_acts + jax.nn.sigmoid(cond_proj[:, 2 * c_token:3 * c_token] + gate_bias[block_idx, 0]) * attn_out
                normed = (jax.nn.sigmoid(cond_proj[:, 3 * c_token:4 * c_token]) * layer_norm(token_acts) + cond_proj[:, 4 * c_token:5 * c_token]).astype(jnp.bfloat16)
                hidden = jnp.dot(normed, w_up[block_idx], preferred_element_type=jnp.float32)
                gated_act = (jax.nn.silu(hidden[:, :2 * c_token]) * hidden[:, 2 * c_token:]).astype(jnp.bfloat16)
                token_acts = token_acts + jax.nn.sigmoid(cond_proj[:, 5 * c_token:] + gate_bias[block_idx, 1]) * jnp.dot(gated_act, w_down[block_idx], preferred_element_type=jnp.float32)
            r_update = jnp.dot(layer_norm(token_acts).astype(jnp.bfloat16), w_out, preferred_element_type=jnp.float32)
            denoised = (SIGMA_DATA * SIGMA_DATA / noise_var) * x_noisy + (t_hat * SIGMA_DATA / jnp.sqrt(noise_var)) * r_update
            x_state = x_noisy + STEP_SCALE * (sigmas[step_idx + 1] - t_hat) * (x_noisy - denoised) / t_hat
        return x_state

    in_specs = (P("tok", None), P("tok", None), P("tok", None, None), P(part_axes, None), P(None, part_axes, None)) + (P(),) * 21
    return jax.shard_map(local_run, mesh=mesh, in_specs=in_specs, out_specs=P(part_axes, None), check_vma=False)
```

profile of v0, /device:TPU:112, one launch (start us, length us, event | category | flops | bytes accessed | tf_op | source)
XLA Modules:
  0.0 320.4 jit_solution(2553454683610452318)
XLA Ops:
  0.0 1.4 fusion.505
  3.4 1.4 fusion.493
  15.5 1.1 add_reduce_fusion
  16.8 1.2 fusion.155
  17.9 1.1 fusion.525
  25.0 25.0 %all_gather.18 = bf16[1024,256]{1,0:T(8,128)(2,1)S(1)} all-gather(bf16[128,256]{1,0:T(8,128)(2,1)S(1)} %slice.567), channel_id=1, replica_groups=mesh['sample'=2,'tok'=8] {'tok'}, dimensions={0}, use_global_device_ids=true | all-gather | bytes 589824 | tf_op jit(solution)/shard_map/all_gather | solution.py:101
  50.3 108.1 %while.11 = (s32[]{:T(128)}, bf16[16,8,1024,8]{2,1,0,3:T(8,128)(2,1)}, s32[16]{0:T(128)S(1)}, bf16[128,1024,16]{1,2,0:T(8,128)(2,1)}, s32[]{:T(128)}, /*index=5*...) while((s32[]{:T(128)}, ...), condition=%wide.region_22.23_spmd.clone, body=%wide.region_13.22_spmd.clone.sunk | while | flops 89784336 | bytes 18174004 | solution.py:54
  51.6 1.0 constant_dynamic-slice_fusion.2
  58.4 1.0 constant_dynamic-slice_fusion.2
  65.2 1.0 constant_dynamic-slice_fusion.2
  71.9 1.0 constant_dynamic-slice_fusion.2
  78.7 1.0 constant_dynamic-slice_fusion.2
  98.9 1.0 constant_dynamic-slice_fusion.2
  112.4 1.0 constant_dynamic-slice_fusion.2
  153.0 1.0 constant_dynamic-slice_fusion.2
  158.5 2.2 fusion.510
  160.8 2.3 fusion.85
  164.7 21.9 %all_gather.19 = bf16[1024,256]{1,0:T(8,128)(2,1)S(1)} all-gather(bf16[128,256]{1,0:T(8,128)(2,1)S(1)} %slice.581), channel_id=1, replica_groups=mesh['sample'=2,'tok'=8] {'tok'}, dimensions={0}, use_global_device_ids=true | all-gather | bytes 589824 | tf_op jit(solution)/shard_map/all_gather | solution.py:101
  187.0 2.2 fusion.516
  189.3 2.3 fusion.86
  197.6 23.6 %all_gather.20 = bf16[1024,256]{1,0:T(8,128)(2,1)S(1)} all-gather(bf16[128,256]{1,0:T(8,128)(2,1)S(1)} %slice.599), channel_id=1, replica_groups=mesh['sample'=2,'tok'=8] {'tok'}, dimensions={0}, use_global_device_ids=true | all-gather | bytes 589824 | tf_op jit(solution)/shard_map/all_gather | solution.py:101
  221.6 2.2 fusion.521
  223.9 2.3 fusion.87
  227.7 22.0 %all_gather.21 = bf16[1024,256]{1,0:T(8,128)(2,1)S(1)} all-gather(bf16[128,256]{1,0:T(8,128)(2,1)S(1)} %slice.612), channel_id=1, replica_groups=mesh['sample'=2,'tok'=8] {'tok'}, dimensions={0}, use_global_device_ids=true | all-gather | bytes 589824 | tf_op jit(solution)/shard_map/all_gather | solution.py:101
  250.0 2.2 fusion.527
  252.3 2.3 fusion.88
  260.0 23.6 %all_gather.22 = bf16[1024,256]{1,0:T(8,128)(2,1)S(1)} all-gather(bf16[128,256]{1,0:T(8,128)(2,1)S(1)} %slice.629), channel_id=1, replica_groups=mesh['sample'=2,'tok'=8] {'tok'}, dimensions={0}, use_global_device_ids=true | all-gather | bytes 589824 | tf_op jit(solution)/shard_map/all_gather | solution.py:101
  283.9 2.2 fusion.532
  286.3 2.3 fusion.89
  290.1 21.8 %all_gather.23 = bf16[1024,256]{1,0:T(8,128)(2,1)S(1)} all-gather(bf16[128,256]{1,0:T(8,128)(2,1)S(1)} %slice.642), channel_id=1, replica_groups=mesh['sample'=2,'tok'=8] {'tok'}, dimensions={0}, use_global_device_ids=true | all-gather | bytes 589824 | tf_op jit(solution)/shard_map/all_gather | solution.py:101
  312.1 2.2 fusion.536
  314.5 2.3 fusion.90
  (629 shorter events, 112.1 us)
Async XLA Ops:
  0.0 15.5 %copy-start = (bf16[256,128]{1,0:T(8,128)(2,1)S(1)}, bf16[256,128]{1,0:T(8,128)(2,1)}, u32[]{:S(2)}) copy-start(bf16[256,128]{1,0:T(8,128)(2,1)} %param.39) | copy-start | bytes 196612
  0.0 19.1 %copy-start.3 = (bf16[2,128,512]{2,1,0:T(8,128)(2,1)S(1)}, bf16[2,128,512]{2,1,0:T(8,128)(2,1)}, u32[]{:S(2)}) copy-start(bf16[2,128,512]{2,1,0:T(8,128)(2,1)} %param.43) | copy-start | bytes 786436
  0.0 19.3 %copy-start.13 = (bf16[2,256,128]{2,1,0:T(8,128)(2,1)S(1)}, bf16[2,256,128]{2,1,0:T(8,128)(2,1)}, u32[]{:S(2)}) copy-start(bf16[2,256,128]{2,1,0:T(8,128)(2,1)} %param.44) | copy-start | bytes 393220
  20.1 3.1 copy-start.10
  20.2 3.1 copy-start.11
  20.2 3.7 %copy-start.8 = (f32[3,128]{1,0:T(4,128)S(1)}, f32[3,128]{1,0:T(4,128)}, u32[]{:S(2)}) copy-start(f32[3,128]{1,0:T(4,128)} %param.45) | copy-start | bytes 4612
  20.2 3.9 %copy-start.5 = (bf16[128,128]{1,0:T(8,128)(2,1)S(1)}, bf16[128,128]{1,0:T(8,128)(2,1)}, u32[]{:S(2)}) copy-start(bf16[128,128]{1,0:T(8,128)(2,1)} %param.46) | copy-start | bytes 98308
  20.5 4.0 %copy-start.1 = (bf16[2,128,768]{2,1,0:T(8,128)(2,1)S(1)}, bf16[2,128,768]{2,1,0:T(8,128)(2,1)}, u32[]{:S(2)}) copy-start(bf16[2,128,768]{2,1,0:T(8,128)(2,1)} %param.47) | copy-start | bytes 1179652
  20.7 4.0 %copy-start.2 = (bf16[2,128,512]{2,1,0:T(8,128)(2,1)S(1)}, bf16[2,128,512]{2,1,0:T(8,128)(2,1)}, u32[]{:S(2)}) copy-start(bf16[2,128,512]{2,1,0:T(8,128)(2,1)} %param.49) | copy-start | bytes 786436
  23.9 26.4 %copy-start.6 = (bf16[2,16,64]{2,1,0:T(8,128)(2,1)S(1)}, bf16[2,16,64]{2,1,0:T(8,128)(2,1)}, u32[]{:S(2)}) copy-start(bf16[2,16,64]{2,1,0:T(8,128)(2,1)} %param.36) | copy-start | bytes 12292
  23.9 26.4 %copy-start.7 = (bf16[2,16,4]{1,2,0:T(4,128)(2,1)S(1)}, bf16[2,16,4]{1,2,0:T(4,128)(2,1)}, u32[]{:S(2)}) copy-start(bf16[2,16,4]{1,2,0:T(4,128)(2,1)} %param.38) | copy-start | bytes 772
  23.9 26.4 %copy-start.16 = (bf16[2,32,16]{1,2,0:T(8,128)(2,1)S(1)}, bf16[2,32,16]{1,2,0:T(8,128)(2,1)}, u32[]{:S(2)}) copy-start(bf16[2,32,16]{1,2,0:T(8,128)(2,1)} %param.37) | copy-start | bytes 6148
  23.9 26.4 %copy-start.17 = (bf16[65,16]{0,1:T(8,128)(2,1)S(1)}, bf16[65,16]{0,1:T(8,128)(2,1)}, u32[]{:S(2)}) copy-start(bf16[65,16]{0,1:T(8,128)(2,1)} %param.34) | copy-start | bytes 6244
  23.9 26.4 %copy-start.18 = (bf16[32,16]{0,1:T(8,128)(2,1)S(1)}, bf16[32,16]{0,1:T(8,128)(2,1)}, u32[]{:S(2)}) copy-start(bf16[32,16]{0,1:T(8,128)(2,1)} %param.35) | copy-start | bytes 3076
  160.8 2.6 copy-start.12
  160.8 2.6 copy-start.15
  160.8 2.9 copy-start.4
  160.8 3.1 copy-start.14
  191.6 4.2 %copy-start.9 = (bf16[128,3]{0,1:T(4,128)(2,1)S(1)}, bf16[128,3]{0,1:T(4,128)(2,1)}, u32[]{:S(2)}) copy-start(bf16[128,3]{0,1:T(4,128)(2,1)} %param.53) | copy-start | bytes 2308
where the time goes:
time: 322 us; the launch traced here: 320 us
  blocking collectives  138 us (43%)
  matrix products  88.8 us (28%)
  local copies, waits for them, and re-layouts  42.9 us (13%)
  other arithmetic  21.1 us (7%)
  between operations  16.8 us (5%)
  loops' own time  12.8 us (4%)
    all_gather x6, blocking collectives, local_run(): kv_all = lax.all_gather(kv_local, 'tok', axis=0, tiled=True)  138 us
    dot_general x38, matrix products, transition(): jnp.dot(layer_norm(values).astype(jnp.bfloat16), w_up_one, preferred_elem...  17.8 us
    dot_general x38, matrix products, transition(): jnp.dot(gated_act, w_down_one, preferred_element_type=jnp.float32)  15.8 us
    dynamic_slice x16, local copies, waits for them, and re-layouts, one_group(): lax.dynamic_slice_in_dim(z_rows, group_idx * row_group, row_group, axis=0)  15.6 us
    dot_general x6, matrix products, local_run(): jnp.einsum('hqk,khd->qhd', attn_probs, value_heads, preferred_element_typ...  13.8 us
    sub x6, matrix products, local_run(): attn_probs = jax.nn.softmax(scores, axis=-1).astype(jnp.bfloat16)  13 us
    another operation x1, loops' own time, pair_bias_rows(): groups = lax.map(one_group, jnp.arange(tok_rows // row_group))  12.8 us
    reduce_sum x90, other arithmetic, layer_norm(): variance = jnp.mean(centered * centered, axis=-1, keepdims=True)  12.5 us

commit v1 on v0

--- a/solution.py
+++ b/solution.py
@@ -1,8 +1,165 @@
 import math
+import functools
 import jax
 import jax.numpy as jnp
 from jax import lax
+from jax.experimental import pallas as pl
+from jax.experimental.pallas import tpu as pltpu
 from jax.sharding import PartitionSpec as P
+
+EPS = 1e-5
+LOG2E = math.log2(math.e)
+
+
+def spread(n, sub):
+    rows = lax.broadcasted_iota(jnp.int32, (n * sub, n), 0)
+    cols = lax.broadcasted_iota(jnp.int32, (n * sub, n), 1)
+    return ((rows >= cols * sub) & (rows < (cols + 1) * sub)).astype(jnp.bfloat16)
+
+
+def expand(weight, sub):
+    n_out, n_in = weight.shape
+    tall = jnp.dot(spread(n_out, sub), weight, preferred_element_type=jnp.float32).astype(jnp.bfloat16)
+    full = lax.dot_general(tall, spread(n_in, sub), (((1,), (1,)), ((), ())), preferred_element_type=jnp.float32)
+    rows = lax.broadcasted_iota(jnp.int32, full.shape, 0) & (sub - 1)
+    cols = lax.broadcasted_iota(jnp.int32, full.shape, 1) & (sub - 1)
+    return jnp.where(rows == cols, full, 0.0).astype(jnp.bfloat16)
+
+
+def norm_major(values, sub):
+    parts = values.reshape(values.shape[0] // sub, sub, values.shape[1])
+    inv = 1.0 / parts.shape[0]
+    centered = parts - jnp.sum(parts, axis=0, keepdims=True) * inv
+    variance = jnp.sum(centered * centered, axis=0, keepdims=True) * inv
+    return (centered * lax.rsqrt(variance + EPS)).reshape(values.shape)
+
+
+def silu(h):
+    half = 0.5 * h
+    return half + half * jnp.tanh(half)
+
+
+def bias_kernel(chunk, tok_name, z_ref, rel_ref, pin_ref, zup_ref, zdown_ref, pb_ref, out_ref, win_s, wup_s, wdown_s, wpb_s, perm_s, rel_s, relsum_s):
+    sub = 8
+    rows, c_pair, n_tok = z_ref.shape[0], z_ref.shape[1], z_ref.shape[2]
+    n_layers = zup_ref.shape[0]
+    n_bins = rel_ref.shape[1]
+    clip = (n_bins - 1) // 2
+    lanes = 128
+    n_var = rel_s.shape[0]
+    tile = c_pair * sub
+    step = pl.program_id(0)
+
+    @pl.when(step == 0)
+    def _():
+        pin = pin_ref[...]
+        win_s[:, :tile] = expand(pin[:, :c_pair], sub)
+        win_s[:, tile:] = expand(pin[:, c_pair:], sub)
+        for layer in range(n_layers):
+            wup_s[layer] = expand(zup_ref[layer], sub)
+            wdown_s[layer] = expand(zdown_ref[layer], sub)
+        wpb_s[...] = expand(pb_ref[...], sub)
+        rows_i = lax.broadcasted_iota(jnp.int32, (tile, tile), 0)
+        cols_i = lax.broadcasted_iota(jnp.int32, (tile, tile), 1)
+        src = (rows_i & (sub - 1)) * c_pair + (rows_i >> 3)
+        perm_s[...] = (src == cols_i).astype(jnp.bfloat16)
+        tall = jnp.dot(spread(c_pair, sub), rel_ref[...], preferred_element_type=jnp.float32).astype(jnp.bfloat16)
+        n_diag = 128
+        tab = jnp.zeros((tile, n_diag), jnp.float32)
+        bin_i = lax.broadcasted_iota(jnp.int32, (n_bins, n_diag), 0)
+        diag_i = lax.broadcasted_iota(jnp.int32, (n_bins, n_diag), 1)
+        row_s = lax.broadcasted_iota(jnp.int32, (tile, n_diag), 0) & (sub - 1)
+        for s in range(sub):
+            pick = (bin_i == jnp.clip(diag_i - (sub - 1) + s, 0, n_bins - 1)).astype(jnp.bfloat16)
+            cand = jnp.dot(tall, pick, preferred_element_type=jnp.float32)
+            tab = jnp.where(row_s == s, cand, tab)
+        tab = tab.astype(jnp.bfloat16)
+
+        def fill(v, carry):
+            delta = sub * (v - 5)
+            k = lax.broadcasted_iota(jnp.int32, (n_diag, lanes), 0)
+            j = lax.broadcasted_iota(jnp.int32, (n_diag, lanes), 1)
+            want = jnp.clip(delta - j + clip + sub - 1, 0, n_bins + sub - 2)
+            plane = jnp.dot(tab, (k == want).astype(jnp.bfloat16), preferred_element_type=jnp.float32)
+            rel_s[v] = plane
+            relsum_s[v] = jnp.sum(plane.reshape(c_pair, sub, lanes), axis=0)
+            return carry
+
+        lax.fori_loop(0, n_var, fill, 0)
+
+    row0 = lax.axis_index(tok_name) * (rows * pl.num_programs(0)) + step * rows
+
+    def body(it, carry):
+        n_chunks = n_tok // chunk
+        group = it // n_chunks
+        col0 = (it % n_chunks) * chunk
+        r0 = group * sub
+        zb = z_ref[pl.ds(r0, sub), :, pl.ds(pl.multiple_of(col0, chunk), chunk)].reshape(tile, chunk)
+        z = jnp.dot(perm_s[...], zb, preferred_element_type=jnp.float32)
+        rels, sums = [], []
+        for part in range(chunk // lanes):
+            delta = row0 + r0 - col0 - part * lanes
+            v = jnp.clip(delta // sub + 5, 0, n_var - 1)
+            rels.append(rel_s[v])
+            sums.append(relsum_s[v])
+        rel = jnp.concatenate(rels, axis=1).reshape(c_pair, sub, chunk)
+        relsum = jnp.concatenate(sums, axis=1)
+        z = z.reshape(c_pair, sub, chunk)
+        inv = 1.0 / (2 * c_pair)
+        mean = (jnp.sum(z, axis=0) + relsum) * inv
+        zc = z - mean
+        rc = rel - mean
+        var = (jnp.sum(zc * zc, axis=0) + jnp.sum(rc * rc, axis=0)) * inv
+        rs = lax.rsqrt(var + EPS)
+        zn = (zc * rs).reshape(tile, chunk).astype(jnp.bfloat16)
+        rn = (rc * rs).reshape(tile, chunk).astype(jnp.bfloat16)
+        cond = jnp.dot(win_s[...], jnp.concatenate([zn, rn], axis=0), preferred_element_type=jnp.float32)
+        for layer in range(n_layers):
+            xn = norm_major(cond, sub).astype(jnp.bfloat16)
+            h = jnp.dot(wup_s[layer], xn, preferred_element_type=jnp.float32)
+            half = h.shape[0] // 2
+            act = (silu(h[:half]) * h[half:]).astype(jnp.bfloat16)
+            cond = cond + jnp.dot(wdown_s[layer], act, preferred_element_type=jnp.float32)
+        xn = norm_major(cond, sub).astype(jnp.bfloat16)
+        bias = jnp.dot(wpb_s[...], xn, preferred_element_type=jnp.float32)
+        bias = bias.astype(jnp.bfloat16).astype(jnp.float32)
+        out_ref[:, pl.ds(pl.multiple_of(r0, sub), sub), pl.ds(pl.multiple_of(col0, chunk), chunk)] = bias.reshape(-1, sub, chunk)
+        return carry
+
+    lax.fori_loop(0, (rows // sub) * (n_tok // chunk), body, 0)
+
+
+def pair_bias(z_rows, relpos_table, w_pair_in, w_z_up, w_z_down, w_pair_bias, chunk=256, rows=16):
+    tok_rows, n_tok, c_pair = z_rows.shape
+    n_blocks, _, n_heads = w_pair_bias.shape
+    n_layers = w_z_up.shape[0]
+    width = w_z_up.shape[2]
+    sub = 8
+    n_var = 26
+    zt = jnp.transpose(z_rows, (0, 2, 1))
+    whole = lambda a: pl.BlockSpec(a.shape, lambda i, n=a.ndim: (0,) * n)
+    ops = [relpos_table.T, w_pair_in.T, jnp.transpose(w_z_up, (0, 2, 1)), jnp.transpose(w_z_down, (0, 2, 1)), jnp.transpose(w_pair_bias, (0, 2, 1)).reshape(n_blocks * n_heads, c_pair)]
+    out = pl.pallas_call(
+        functools.partial(bias_kernel, chunk, "tok"),
+        grid=(tok_rows // rows,),
+        in_specs=[pl.BlockSpec((rows, c_pair, n_tok), lambda i: (i, 0, 0))] + [whole(a) for a in ops],
+        out_specs=pl.BlockSpec((n_blocks * n_heads, rows, n_tok), lambda i: (0, i, 0)),
+        out_shape=jax.ShapeDtypeStruct((n_blocks * n_heads, tok_rows, n_tok), jnp.float32),
+        scratch_shapes=[
+            pltpu.VMEM((c_pair * sub, 2 * c_pair * sub), jnp.bfloat16),
+            pltpu.VMEM((n_layers, width * sub, c_pair * sub), jnp.bfloat16),
+            pltpu.VMEM((n_layers, c_pair * sub, width // 2 * sub), jnp.bfloat16),
+            pltpu.VMEM((n_blocks * n_heads * sub, c_pair * sub), jnp.bfloat16),
+            pltpu.VMEM((c_pair * sub, c_pair * sub), jnp.bfloat16),
+            pltpu.VMEM((n_var, c_pair * sub, 128), jnp.float32),
+            pltpu.VMEM((n_var, sub, 128), jnp.float32),
+        ],
+        compiler_params=pltpu.CompilerParams(dimension_semantics=("arbitrary",), vmem_limit_bytes=48 * 1024 * 1024),
+        cost_estimate=pl.CostEstimate(flops=10**10, bytes_accessed=10**7, transcendentals=10**7),
+        name="pair_bias",
+    )(zt, *ops)
+    return out.reshape(n_blocks, n_heads, tok_rows, n_tok)
+
 
 SIGMA_DATA = 16.0
 GAMMA = 0.8
@@ -23,37 +180,6 @@
     half_width = hidden.shape[-1] // 2
     gated_act = (jax.nn.silu(hidden[..., :half_width]) * hidden[..., half_width:]).astype(jnp.bfloat16)
     return values + jnp.dot(gated_act, w_down_one, preferred_element_type=jnp.float32)
-
-
-def pair_bias_rows(z_rows, row_start, relpos_table, w_pair_in, w_z_up, w_z_down, w_pair_bias):
-    tok_rows = z_rows.shape[0]
-    n_tok = z_rows.shape[1]
-    c_pair = z_rows.shape[2]
-    n_blocks = w_pair_bias.shape[0]
-    n_heads = w_pair_bias.shape[2]
-    n_bins = relpos_table.shape[0]
-    rel_clip = (n_bins - 1) // 2
-    row_group = 8
-    bias_weight = jnp.transpose(w_pair_bias, (1, 0, 2)).reshape(c_pair, n_blocks * n_heads)
-    bin_ids = jnp.arange(n_bins)
-    col_ids = jnp.arange(n_tok)
-
-    def one_group(group_idx):
-        z_group = lax.dynamic_slice_in_dim(z_rows, group_idx * row_group, row_group, axis=0)
-        row_ids = row_start + group_idx * row_group + jnp.arange(row_group)
-        bin_index = jnp.clip(row_ids[:, None] - col_ids[None, :] + rel_clip, 0, n_bins - 1)
-        one_hot = (bin_index[:, :, None] == bin_ids).astype(jnp.bfloat16)
-        rel_feat = jnp.dot(one_hot, relpos_table, preferred_element_type=jnp.float32).astype(jnp.bfloat16)
-        pair_in = layer_norm(jnp.concatenate([z_group, rel_feat], axis=-1)).astype(jnp.bfloat16)
-        pair_cond = jnp.dot(pair_in, w_pair_in, preferred_element_type=jnp.float32)
-        for layer_idx in range(w_z_up.shape[0]):
-            pair_cond = transition(pair_cond, w_z_up[layer_idx], w_z_down[layer_idx])
-        bias_flat = jnp.dot(layer_norm(pair_cond).astype(jnp.bfloat16), bias_weight, preferred_element_type=jnp.float32)
-        return bias_flat.astype(jnp.bfloat16)
-
-    groups = lax.map(one_group, jnp.arange(tok_rows // row_group))
-    bias_rows = groups.reshape(tok_rows, n_tok, n_blocks, n_heads)
-    return jnp.transpose(bias_rows, (2, 3, 0, 1))
 
 
 def single_cond(s_base, t_hat, fourier_w, fourier_b, w_fourier, w_s_up, w_s_down):
@@ -78,8 +204,7 @@
         n_heads = w_pair_bias.shape[2]
         head_dim = c_token // n_heads
         score_scale = head_dim ** -0.5
-        row_start = lax.axis_index("tok") * tok_rows
-        bias_all = pair_bias_rows(z_trunk, row_start, relpos_table, w_pair_in, w_z_up, w_z_down, w_pair_bias)
+        bias_all = pair_bias(z_trunk, relpos_table, w_pair_in, w_z_up, w_z_down, w_pair_bias)
         key_valid = jnp.arange(n_tok) < n_valid
         joined = layer_norm(jnp.concatenate([s_trunk, s_inputs], axis=-1)).astype(jnp.bfloat16)
         s_base = jnp.dot(joined, w_single, preferred_element_type=jnp.float32)

time: 322 us -> 354 us (1.099)
  Pallas kernels: 0 us -> 101 us
  matrix products: 88.8 us -> 58 us
  local copies, waits for them, and re-layouts: 42.9 us -> 19.8 us
  loops' own time: 12.8 us -> 0 us
    pallas_call x0 -> x1, Pallas kernels: none -> 101 us  [pair_bias(): pl.pallas_call(functools.partial(bias_kernel, chunk, 'tok'), grid=(tok_ro...]
    dynamic_slice x32 -> x0, local copies, waits for them, and re-layouts: 25.7 us -> none  [the longest x16 15.6 us: one_group(): lax.dynamic_slice_in_dim(z_rows, group_idx * row_group, row_group, axis=0)]
    dot_general x38 -> x6, matrix products: 17.8 us -> 2.37 us  [transition(): jnp.dot(layer_norm(values).astype(jnp.bfloat16), w_up_one, preferred_elem...]
    dot_general x38 -> x6, matrix products: 15.8 us -> 2.22 us  [transition(): jnp.dot(gated_act, w_down_one, preferred_element_type=jnp.float32)]
    sub x6 -> x0, matrix products: 13 us -> none  [local_run(): attn_probs = jax.nn.softmax(scores, axis=-1).astype(jnp.bfloat16)]
    another operation x1 -> x0, loops' own time: 12.8 us -> none  [pair_bias_rows(): groups = lax.map(one_group, jnp.arange(tok_rows // row_group))]
    dynamic_update_slice x16 -> x0, local copies, waits for them, and re-layouts: 12 us -> none  [pair_bias_rows(): groups = lax.map(one_group, jnp.arange(tok_rows // row_group))]
    reduce_sum x90 -> x26, other arithmetic: 12.5 us -> 3.75 us  [layer_norm(): variance = jnp.mean(centered * centered, axis=-1, keepdims=True)]
where the time goes in v1:
time: 354 us; the launch traced here: 352 us
  blocking collectives  138 us (39%)
  Pallas kernels  101 us (29%)
  matrix products  58 us (16%)
  local copies, waits for them, and re-layouts  19.8 us (6%)
  other arithmetic  17.8 us (5%)
  between operations  16.8 us (5%)
    all_gather x6, blocking collectives, local_run(): kv_all = lax.all_gather(kv_local, 'tok', axis=0, tiled=True)  138 us
    pallas_call x1, Pallas kernels, pair_bias(): pl.pallas_call(functools.partial(bias_kernel, chunk, 'tok'), grid=(tok_ro...  101 us
    dot_general x6, matrix products, local_run(): jnp.einsum('hqk,khd->qhd', attn_probs, value_heads, preferred_element_typ...  14.7 us
    dot_general x6, matrix products, local_run(): jnp.einsum('qhd,khd->hqk', query_heads, key_heads, preferred_element_type...  11.1 us

profile of v1, /device:TPU:112, one launch (start us, length us, event | category | flops | bytes accessed | tf_op | source)
XLA Modules:
  0.0 351.8 jit_solution(10300309939659585190)
XLA Ops:
  0.0 1.5 fusion.410
  3.5 1.4 fusion.401
  16.7 1.2 fusion.105
  17.9 1.1 fusion.430
  24.5 1.3 broadcast_divide_fusion.2
  27.7 25.0 %all_gather.18 = bf16[1024,256]{1,0:T(8,128)(2,1)S(1)} all-gather(bf16[128,256]{1,0:T(8,128)(2,1)S(1)} %slice.533), channel_id=1, replica_groups=mesh['sample'=2,'tok'=8] {'tok'}, dimensions={0}, use_global_device_ids=true | all-gather | bytes 589824 | tf_op jit(solution)/shard_map/all_gather | solution.py:226
  53.1 101.5 %pair_bias.1 = f32[8,128,1024]{2,1,0:T(8,128)S(1)} custom-call(bf16[128,16,1024]{2,1,0:T(8,128)(2,1)} %bitcast.317, bf16[16,65]{1,0:T(8,128)(2,1)S(1)} %bitcast.296, bf16[16,32]{1,0:T(8,128)(2,1)S(1)} %bitcast.297, bf16[2,64,16]{2,1,0:T(8,128)(2,1)S(1)} %bitcast.294, bf16[2,16,32]{2,1,0:T(8,128)(2,1)S(1)} %bitcast.295, bf16[8,16]{1,0:T(8,128)(2,1)S(1)} %bitcast.298), custom_call_target="tpu_custom_call" | custom-call | flops 10000000000 | bytes 10000000 | tf_op jit(solution)/shard_map/pair_bias/pallas_call | solution.py:142
  155.1 1.4 copy-done.1
  157.9 2.7 fusion.35
  164.4 1.1 fusion.417
  166.7 21.9 %all_gather.19 = bf16[1024,256]{1,0:T(8,128)(2,1)S(1)} all-gather(bf16[128,256]{1,0:T(8,128)(2,1)S(1)} %slice.547), channel_id=1, replica_groups=mesh['sample'=2,'tok'=8] {'tok'}, dimensions={0}, use_global_device_ids=true | all-gather | bytes 589824 | tf_op jit(solution)/shard_map/all_gather | solution.py:226
  189.7 2.1 add_select_fusion.4
  193.6 2.7 fusion.36
  199.5 1.1 fusion.423
  204.0 1.5 broadcast_divide_fusion.1
  207.3 23.6 %all_gather.20 = bf16[1024,256]{1,0:T(8,128)(2,1)S(1)} all-gather(bf16[128,256]{1,0:T(8,128)(2,1)S(1)} %slice.565), channel_id=1, replica_groups=mesh['sample'=2,'tok'=8] {'tok'}, dimensions={0}, use_global_device_ids=true | all-gather | bytes 589824 | tf_op jit(solution)/shard_map/all_gather | solution.py:226
  231.9 2.1 add_select_fusion.3
  234.1 1.1 fusion.426
  236.0 2.7 fusion.37
  241.9 1.1 fusion.428
  244.2 22.0 %all_gather.21 = bf16[1024,256]{1,0:T(8,128)(2,1)S(1)} all-gather(bf16[128,256]{1,0:T(8,128)(2,1)S(1)} %slice.578), channel_id=1, replica_groups=mesh['sample'=2,'tok'=8] {'tok'}, dimensions={0}, use_global_device_ids=true | all-gather | bytes 589824 | tf_op jit(solution)/shard_map/all_gather | solution.py:226
  267.2 2.1 add_select_fusion.2
  271.3 2.7 fusion.38
  277.1 1.1 fusion.434
  281.4 1.4 broadcast_divide_fusion
  284.6 23.6 %all_gather.22 = bf16[1024,256]{1,0:T(8,128)(2,1)S(1)} all-gather(bf16[128,256]{1,0:T(8,128)(2,1)S(1)} %slice.595), channel_id=1, replica_groups=mesh['sample'=2,'tok'=8] {'tok'}, dimensions={0}, use_global_device_ids=true | all-gather | bytes 589824 | tf_op jit(solution)/shard_map/all_gather | solution.py:226
  309.2 2.1 add_select_fusion.1
  313.2 2.7 fusion.39
  319.0 1.1 fusion.439
  321.4 21.7 %all_gather.23 = bf16[1024,256]{1,0:T(8,128)(2,1)S(1)} all-gather(bf16[128,256]{1,0:T(8,128)(2,1)S(1)} %slice.608), channel_id=1, replica_groups=mesh['sample'=2,'tok'=8] {'tok'}, dimensions={0}, use_global_device_ids=true | all-gather | bytes 589824 | tf_op jit(solution)/shard_map/all_gather | solution.py:226
  343.4 2.1 add_select_fusion
  346.2 1.1 fusion.40
  (294 shorter events, 53.1 us)
Async XLA Ops:
  0.0 15.5 %copy-start = (bf16[256,128]{1,0:T(8,128)(2,1)S(1)}, bf16[256,128]{1,0:T(8,128)(2,1)}, u32[]{:S(2)}) copy-start(bf16[256,128]{1,0:T(8,128)(2,1)} %param.37) | copy-start | bytes 196612
  0.0 19.1 %copy-start.8 = (bf16[2,128,512]{2,1,0:T(8,128)(2,1)S(1)}, bf16[2,128,512]{2,1,0:T(8,128)(2,1)}, u32[]{:S(2)}) copy-start(bf16[2,128,512]{2,1,0:T(8,128)(2,1)} %param.41) | copy-start | bytes 786436
  0.0 19.3 %copy-start.46 = (bf16[2,256,128]{2,1,0:T(8,128)(2,1)S(1)}, bf16[2,256,128]{2,1,0:T(8,128)(2,1)}, u32[]{:S(2)}) copy-start(bf16[2,256,128]{2,1,0:T(8,128)(2,1)} %param.42) | copy-start | bytes 393220
  20.8 5.1 %copy-start.33 = (f32[3,128]{1,0:T(4,128)S(1)}, f32[3,128]{1,0:T(4,128)}, u32[]{:S(2)}) copy-start(f32[3,128]{1,0:T(4,128)} %param.43) | copy-start | bytes 4612
  20.8 5.3 %copy-start.30 = (bf16[128,128]{1,0:T(8,128)(2,1)S(1)}, bf16[128,128]{1,0:T(8,128)(2,1)}, u32[]{:S(2)}) copy-start(bf16[128,128]{1,0:T(8,128)(2,1)} %param.44) | copy-start | bytes 98308
  21.0 5.4 %copy-start.6 = (bf16[2,128,768]{2,1,0:T(8,128)(2,1)S(1)}, bf16[2,128,768]{2,1,0:T(8,128)(2,1)}, u32[]{:S(2)}) copy-start(bf16[2,128,768]{2,1,0:T(8,128)(2,1)} %param.45) | copy-start | bytes 1179652
  21.3 5.4 %copy-start.7 = (bf16[2,128,512]{2,1,0:T(8,128)(2,1)S(1)}, bf16[2,128,512]{2,1,0:T(8,128)(2,1)}, u32[]{:S(2)}) copy-start(bf16[2,128,512]{2,1,0:T(8,128)(2,1)} %param.47) | copy-start | bytes 786436
  23.1 29.9 %copy-start.28 = (bf16[128,128]{0,1:T(8,128)(2,1)}, bf16[128,128]{0,1:T(8,128)(2,1)S(1)}, u32[]{:S(2)}) copy-start(bf16[128,128]{0,1:T(8,128)(2,1)S(1)} %multiply_convert_fusion.9) | copy-start | bytes 98308
  24.5 28.5 %copy-start.35 = (bf16[2,16,64]{2,1,0:T(8,128)(2,1)S(1)}, bf16[2,16,64]{2,1,0:T(8,128)(2,1)}, u32[]{:S(2)}) copy-start(bf16[2,16,64]{2,1,0:T(8,128)(2,1)} %param.34) | copy-start | bytes 12292
  26.0 27.1 %copy-start.2 = (bf16[2,32,16]{1,2,0:T(8,128)(2,1)S(1)}, bf16[2,32,16]{1,2,0:T(8,128)(2,1)}, u32[]{:S(2)}) copy-start(bf16[2,32,16]{1,2,0:T(8,128)(2,1)} %param.35) | copy-start | bytes 6148
  26.0 27.1 %copy-start.3 = (bf16[65,16]{0,1:T(8,128)(2,1)S(1)}, bf16[65,16]{0,1:T(8,128)(2,1)}, u32[]{:S(2)}) copy-start(bf16[65,16]{0,1:T(8,128)(2,1)} %param.32) | copy-start | bytes 6244
  26.0 27.1 %copy-start.4 = (bf16[32,16]{0,1:T(8,128)(2,1)S(1)}, bf16[32,16]{0,1:T(8,128)(2,1)}, u32[]{:S(2)}) copy-start(bf16[32,16]{0,1:T(8,128)(2,1)} %param.33) | copy-start | bytes 3076
  26.0 27.1 %copy-start.5 = (bf16[2,16,4]{1,2,0:T(4,128)(2,1)S(1)}, bf16[2,16,4]{1,2,0:T(4,128)(2,1)}, u32[]{:S(2)}) copy-start(bf16[2,16,4]{1,2,0:T(4,128)(2,1)} %param.36) | copy-start | bytes 772
  157.9 4.6 %copy-start.39 = (f32[2,2,128]{2,1,0:T(2,128)S(1)}, f32[2,2,128]{2,1,0:T(2,128)}, u32[]{:S(2)}) copy-start(f32[2,2,128]{2,1,0:T(2,128)} %param.46) | copy-start | bytes 6148
  157.9 5.2 %copy-start.15 = (f32[128,768]{0,1:T(8,128)S(1)}, f32[128,768]{0,1:T(8,128)}, u32[]{:S(2)}) copy-start(f32[128,768]{0,1:T(8,128)} %copy-done.14) | copy-start | bytes 1179652
  157.9 6.2 %copy-start.9 = (bf16[2,128,512]{2,1,0:T(8,128)(2,1)S(1)}, bf16[2,128,512]{2,1,0:T(8,128)(2,1)}, u32[]{:S(2)}) copy-start(bf16[2,128,512]{2,1,0:T(8,128)(2,1)} %param.49) | copy-start | bytes 786436
  160.6 4.9 %copy-start.29 = (bf16[128,128]{0,1:T(8,128)(2,1)S(1)}, bf16[128,128]{0,1:T(8,128)(2,1)}, u32[]{:S(2)}) copy-start(bf16[128,128]{0,1:T(8,128)(2,1)} %copy-done.28) | copy-start | bytes 98308
  163.1 26.3 %copy-start.43 = (f32[128]{0:T(128)}, f32[128]{0:T(128)S(1)}, u32[]{:S(2)}) copy-start(f32[128]{0:T(128)S(1)} %get-tuple-element.30) | copy-start | bytes 1540
  193.6 4.6 %copy-start.17 = (f32[128,768]{0,1:T(8,128)S(1)}, f32[128,768]{0,1:T(8,128)}, u32[]{:S(2)}) copy-start(f32[128,768]{0,1:T(8,128)} %copy-done.16) | copy-start | bytes 1179652
  193.6 5.9 %copy-start.40 = (f32[128]{0:T(128)S(1)}, f32[128]{0:T(128)}, u32[]{:S(2)}) copy-start(f32[128]{0:T(128)} %get-tuple-element.29) | copy-start | bytes 1540
  196.3 7.7 %copy-start.34 = (bf16[128,3]{0,1:T(4,128)(2,1)S(1)}, bf16[128,3]{0,1:T(4,128)(2,1)}, u32[]{:S(2)}) copy-start(bf16[128,3]{0,1:T(4,128)(2,1)} %param.51) | copy-start | bytes 2308
  196.3 7.7 %copy-start.38 = (f32[128,3]{0,1:T(4,128)S(1)}, f32[128,3]{0,1:T(4,128)}, u32[]{:S(2)}) copy-start(f32[128,3]{0,1:T(4,128)} %param.29) | copy-start | bytes 4612
  196.3 9.4 %copy-start.26 = (bf16[128,128]{0,1:T(8,128)(2,1)S(1)}, bf16[128,128]{0,1:T(8,128)(2,1)}, u32[]{:S(2)}) copy-start(bf16[128,128]{0,1:T(8,128)(2,1)} %multiply_convert_fusion.5) | copy-start | bytes 98308
  196.4 9.4 %copy-start.31 = (bf16[128,128]{1,0:T(8,128)(2,1)S(1)}, bf16[128,128]{1,0:T(8,128)(2,1)}, u32[]{:S(2)}) copy-start(bf16[128,128]{1,0:T(8,128)(2,1)} %param.44) | copy-start | bytes 98308
  236.0 4.6 %copy-start.23 = (f32[128,768]{0,1:T(8,128)S(1)}, f32[128,768]{0,1:T(8,128)}, u32[]{:S(2)}) copy-start(f32[128,768]{0,1:T(8,128)} %copy-done.22) | copy-start | bytes 1179652
  238.7 4.2 %copy-start.27 = (bf16[128,128]{0,1:T(8,128)(2,1)S(1)}, bf16[128,128]{0,1:T(8,128)(2,1)}, u32[]{:S(2)}) copy-start(bf16[128,128]{0,1:T(8,128)(2,1)} %multiply_convert_fusion.5) | copy-start | bytes 98308
  271.3 4.6 %copy-start.21 = (f32[128,768]{0,1:T(8,128)S(1)}, f32[128,768]{0,1:T(8,128)}, u32[]{:S(2)}) copy-start(f32[128,768]{0,1:T(8,128)} %copy-done.20) | copy-start | bytes 1179652
  274.0 9.0 %copy-start.24 = (bf16[128,128]{0,1:T(8,128)(2,1)S(1)}, bf16[128,128]{0,1:T(8,128)(2,1)}, u32[]{:S(2)}) copy-start(bf16[128,128]{0,1:T(8,128)(2,1)} %multiply_convert_fusion.1) | copy-start | bytes 98308
  274.0 9.0 %copy-start.32 = (bf16[128,128]{1,0:T(8,128)(2,1)S(1)}, bf16[128,128]{1,0:T(8,128)(2,1)}, u32[]{:S(2)}) copy-start(bf16[128,128]{1,0:T(8,128)(2,1)} %param.44) | copy-start | bytes 98308
  313.2 4.6 %copy-start.19 = (f32[128,768]{0,1:T(8,128)S(1)}, f32[128,768]{0,1:T(8,128)}, u32[]{:S(2)}) copy-start(f32[128,768]{0,1:T(8,128)} %copy-done.18) | copy-start | bytes 1179652
  313.2 5.8 %copy-start.44 = (f32[128]{0:T(128)S(1)}, f32[128]{0:T(128)}, u32[]{:S(2)}) copy-start(f32[128]{0:T(128)} %copy-done.43) | copy-start | bytes 1540
  315.9 4.3 %copy-start.25 = (bf16[128,128]{0,1:T(8,128)(2,1)S(1)}, bf16[128,128]{0,1:T(8,128)(2,1)}, u32[]{:S(2)}) copy-start(bf16[128,128]{0,1:T(8,128)(2,1)} %multiply_convert_fusion.1) | copy-start | bytes 98308
  (17 other events, 28.9 us)

commit v2 on v0

v2 whole, which is shorter than its diff:
```python
import functools
import math
import jax
import jax.numpy as jnp
from jax import lax
from jax.experimental import pallas as pl
from jax.experimental.pallas import tpu as pltpu
from jax.sharding import PartitionSpec as P

SIGMA_DATA = 16.0
GAMMA = 0.8
NOISE_SCALE = 1.003
STEP_SCALE = 1.5
MASK_VALUE = -1e9
EPS = 1e-5
LOG2E = math.log2(math.e)
LANES = 128
SUB = 8
CHUNK = 256
F32 = jnp.float32
BF16 = jnp.bfloat16


def dot(a, b):
    return jnp.dot(a, b, preferred_element_type=F32)


def dot_t(a, b):
    return lax.dot_general(a, b, (((1,), (1,)), ((), ())), preferred_element_type=F32)


def spread(n):
    rows = lax.broadcasted_iota(jnp.int32, (n * SUB, n), 0)
    cols = lax.broadcasted_iota(jnp.int32, (n * SUB, n), 1)
    return (rows // SUB == cols).astype(BF16)


def expand_tall(tall):
    full = dot_t(tall.astype(BF16), spread(tall.shape[1]))
    rows = lax.broadcasted_iota(jnp.int32, full.shape, 0) & (SUB - 1)
    cols = lax.broadcasted_iota(jnp.int32, full.shape, 1) & (SUB - 1)
    return jnp.where(rows == cols, full, 0.0)


def expand(weight):
    return expand_tall(dot(spread(weight.shape[0]), weight)).astype(BF16)


def norm_major(values):
    parts = values.reshape(values.shape[0] // SUB, SUB, values.shape[1])
    inv = 1.0 / parts.shape[0]
    centered = parts - jnp.sum(parts, axis=0, keepdims=True) * inv
    variance = jnp.sum(centered * centered, axis=0, keepdims=True) * inv
    return (centered * lax.rsqrt(variance + EPS)).reshape(values.shape).astype(BF16)


def norm_rows(values):
    inv = 1.0 / values.shape[-1]
    centered = values - jnp.sum(values, axis=-1, keepdims=True) * inv
    variance = jnp.sum(centered * centered, axis=-1, keepdims=True) * inv
    return centered * lax.rsqrt(variance + EPS)


def sigmoid(h):
    return 0.5 + 0.5 * jnp.tanh(0.5 * h)


def silu(h):
    half = 0.5 * h
    return half + half * jnp.tanh(half)


def kernel(
    axis, n_peers,
    sig_ref, z_hbm, rel_ref, pin_ref, zup_ref, zdown_ref, pb_ref,
    st_ref, si_ref, x_ref, noise_ref, wsingle_ref, fw_ref, fb_ref, wfour_ref, wsup_ref, wsdown_ref,
    win_ref, wstok_ref, wcond_ref, gbias_ref, wqkvg_ref, wao_ref, wup_ref, wdown_ref, wout_ref,
    out_ref,
    z_s, bias_s, pwin_s, pwup_s, pwdown_s, pwpb_s, perm_s, rel_s, relsum_s,
    zp_s, cond_ss, held_ss, act_ss,
    base_s, four_s, astok_s, gate_s, acts_s, xs_s, y_s,
    z_sem, send_sem, recv_sem,
):
    me = lax.axis_index(axis)
    tok_rows, c_pair, n_tok = z_hbm.shape
    n_layers = zup_ref.shape[0]
    n_bins = rel_ref.shape[1]
    clip = (n_bins - 1) // 2
    n_blocks, n_heads = pb_ref.shape[0], pb_ref.shape[1]
    c_token = st_ref.shape[1]
    head_dim = c_token // n_heads
    n_steps = noise_ref.shape[0]
    n_valid = n_tok - tok_rows // 4
    tile = c_pair * SUB
    n_var = rel_s.shape[0]
    low = (clip + SUB) // SUB

    z_copy = pltpu.make_async_copy(z_hbm, z_s, z_sem)
    z_copy.start()
    barrier = pltpu.get_barrier_semaphore()
    for off in range(1, n_peers):
        pl.semaphore_signal(barrier, inc=1, device_id={axis: lax.rem(me + off, n_peers)}, device_id_type=pl.DeviceIdType.MESH)

    row = lax.broadcasted_iota(jnp.int32, (SUB, 1), 0)
    t_col = jnp.full((SUB, 1), sig_ref[0] * (1.0 + GAMMA), F32)
    for k in range(1, n_steps):
        t_col = jnp.where(row == k, sig_ref[k] * (1.0 + GAMMA), t_col)
    level = 0.25 * jnp.log(t_col / SIGMA_DATA)
    feat = jnp.cos(2.0 * math.pi * (level * fw_ref[...] + fb_ref[...]))
    four_s[...] = dot(norm_rows(feat).astype(BF16), wfour_ref[...])
    joined = norm_rows(jnp.concatenate([st_ref[...].astype(F32), si_ref[...].astype(F32)], axis=-1)).astype(BF16)
    base_s[...] = dot(joined, wsingle_ref[...])

    def condition(k):
        single = base_s[...] + four_s[pl.ds(k, 1), :]
        for layer in range(wsup_ref.shape[0]):
            h = dot(norm_rows(single).astype(BF16), wsup_ref[layer])
            half = h.shape[1] // 2
            act = (silu(h[:, :half]) * h[:, half:]).astype(BF16)
            single = single + dot(act, wsdown_ref[layer])
        u = norm_rows(single).astype(BF16)
        astok_s[k] = dot(u, wstok_ref[...])
        for b in range(n_blocks):
            cond = dot(u, wcond_ref[b])
            part = lambda i: cond[:, i * c_token:(i + 1) * c_token]
            gate_s[k, b, 0] = sigmoid(part(0))
            gate_s[k, b, 1] = part(1)
            gate_s[k, b, 2] = sigmoid(part(2) + gbias_ref[b, 0:1, :])
            gate_s[k, b, 3] = sigmoid(part(3))
            gate_s[k, b, 4] = part(4)
            gate_s[k, b, 5] = sigmoid(part(5) + gbias_ref[b, 1:2, :])

    def copies(r):
        out = []
        for off in range(1, n_peers):
            peer = lax.rem(me + off, n_peers)
            out.append(pltpu.make_async_remote_copy(
                src_ref=y_s.at[r, me], dst_ref=y_s.at[r, me],
                send_sem=send_sem.at[r, off - 1], recv_sem=recv_sem.at[r, off - 1],
                device_id={axis: peer}, device_id_type=pl.DeviceIdType.MESH))
        return out

    def noisy(k):
        c = jnp.full((1, tok_rows), sig_ref[k], F32)
        t = c * (1.0 + GAMMA)
        xn = xs_s[...] + NOISE_SCALE * jnp.sqrt(t * t - c * c) * noise_ref[k]
        return xn, t, t * t + SIGMA_DATA * SIGMA_DATA

    def begin(k):
        xn, t, var = noisy(k)
        r = xn / jnp.sqrt(var)
        cols = jnp.transpose(jnp.concatenate([r, jnp.zeros((SUB - r.shape[0], r.shape[1]), F32)], axis=0))
        acts = astok_s[k]
        lin = cols[:, 0:1] * win_ref[0:1, :]
        for d in range(1, r.shape[0]):
            lin = lin + cols[:, d:d + 1] * win_ref[d:d + 1, :]
        acts_s[...] = lin + acts

    def send(k, b, r):
        y = (gate_s[k, b, 0] * norm_rows(acts_s[...]) + gate_s[k, b, 1]).astype(BF16)
        y_s[r, me] = y
        for copy in copies(r):
            copy.start()

    condition(0)
    xs_s[...] = sig_ref[0] * x_ref[...]
    begin(0)
    pl.semaphore_wait(barrier, n_peers - 1)
    send(0, 0, 0)

    pin = pin_ref[...]
    pwin_s[:, :tile] = expand(pin[:, :c_pair])
    pwin_s[:, tile:] = expand(pin[:, c_pair:])
    for layer in range(n_layers):
        up = zup_ref[layer]
        width = up.shape[1]
        full = expand_tall(dot_t(spread(width), up))
        gate_rows = lax.broadcasted_iota(jnp.int32, full.shape, 0) < (width // 2) * SUB
        pwup_s[layer] = jnp.where(gate_rows, 0.5 * full, full).astype(BF16)
        pwdown_s[layer] = expand(zdown_ref[layer])
    for b in range(n_blocks):
        pwpb_s[b * n_heads * SUB:(b + 1) * n_heads * SUB, :] = expand(pb_ref[b])
    rows_i = lax.broadcasted_iota(jnp.int32, (tile, tile), 0)
    cols_i = lax.broadcasted_iota(jnp.int32, (tile, tile), 1)
    perm_s[...] = ((rows_i & (SUB - 1)) * c_pair + rows_i // SUB == cols_i).astype(BF16)
    tall = dot(spread(c_pair), rel_ref[...]).astype(BF16)
    bin_i = lax.broadcasted_iota(jnp.int32, (n_bins, LANES), 0)
    diag_i = lax.broadcasted_iota(jnp.int32, (n_bins, LANES), 1)
    row_s = lax.broadcasted_iota(jnp.int32, (tile, LANES), 0) & (SUB - 1)
    tab = jnp.zeros((tile, LANES), F32)
    for s in range(SUB):
        pick = (bin_i == jnp.clip(diag_i - (SUB - 1) + s, 0, n_bins - 1)).astype(BF16)
        tab = jnp.where(row_s == s, dot(tall, pick), tab)
    tab = tab.astype(BF16)

    per = 2
    k_i = lax.broadcasted_iota(jnp.int32, (LANES, LANES), 0)
    j_i = lax.broadcasted_iota(jnp.int32, (LANES, LANES), 1)

    def fill(i, carry):
        picks = []
        for p in range(per):
            delta = SUB * (i * per + p - low)
            want = jnp.clip(delta - j_i + clip + SUB - 1, 0, n_bins + SUB - 2)
            picks.append((k_i == want).astype(BF16))
        planes = dot(tab, jnp.concatenate(picks, axis=1))
        for p in range(per):
            plane = planes[:, p * LANES:(p + 1) * LANES]
            rel_s[i * per + p] = plane
            relsum_s[i * per + p] = jnp.sum(plane.reshape(c_pair, SUB, LANES), axis=0)
        return carry

    lax.fori_loop(0, n_var // per, fill, 0)
    z_copy.wait()

    n_chunks = n_tok // CHUNK
    total = (tok_rows // SUB) * n_chunks
    depth = 2 + 2 * n_layers

    def place(it, lag):
        idx = jnp.clip(it - lag, 0, total - 1)
        return (idx // n_chunks) * SUB, (idx % n_chunks) * CHUNK

    def trip(it, carry):
        r0, c0 = place(it, depth)
        bias = dot(pwpb_s[...], norm_major(cond_ss[n_layers]))
        bias = bias.astype(BF16).astype(F32) * LOG2E
        bias_s[:, pl.ds(pl.multiple_of(r0, SUB), SUB), pl.ds(pl.multiple_of(c0, CHUNK), CHUNK)] = bias.reshape(n_blocks * n_heads, SUB, CHUNK)
        for layer in reversed(range(n_layers)):
            cond_ss[layer + 1] = held_ss[layer] + dot(pwdown_s[layer], act_ss[layer])
            cond = cond_ss[layer]
            h = dot(pwup_s[layer], norm_major(cond))
            half = h.shape[0] // 2
            gate = h[:half]
            act_ss[layer] = ((gate + gate * jnp.tanh(gate)) * h[half:]).astype(BF16)
            held_ss[layer] = cond
        r0, c0 = place(it, 1)
        z = zp_s[...].reshape(c_pair, SUB, CHUNK)
        rels, sums = [], []
        for part in range(CHUNK // LANES):
            delta = me * tok_rows + r0 - c0 - part * LANES
            v = jnp.clip(delta // SUB + low, 0, n_var - 1)
            rels.append(rel_s[v])
            sums.append(relsum_s[v])
        rel = jnp.concatenate(rels, axis=1).reshape(c_pair, SUB, CHUNK)
        inv = 1.0 / (2 * c_pair)
        mean = (jnp.sum(z, axis=0) + jnp.concatenate(sums, axis=1)) * inv
        zc = z - mean
        rc = rel - mean
        var = (jnp.sum(zc * zc, axis=0) + jnp.sum(rc * rc, axis=0)) * inv
        rs = lax.rsqrt(var + EPS)
        zn = (zc * rs).reshape(tile, CHUNK).astype(BF16)
        rn = (rc * rs).reshape(tile, CHUNK).astype(BF16)
        cond_ss[0] = dot(pwin_s[...], jnp.concatenate([zn, rn], axis=0))
        r0, c0 = place(it, 0)
        zb = z_s[pl.ds(r0, SUB), :, pl.ds(pl.multiple_of(c0, CHUNK), CHUNK)].reshape(tile, CHUNK)
        zp_s[...] = dot(perm_s[...], zb)
        return carry

    zp_s[...] = jnp.zeros(zp_s.shape, F32)
    cond_ss[...] = jnp.zeros(cond_ss.shape, F32)
    held_ss[...] = jnp.zeros(held_ss.shape, F32)
    act_ss[...] = jnp.zeros(act_ss.shape, BF16)
    lax.fori_loop(0, total + depth, trip, 0)

    lane = lax.broadcasted_iota(jnp.int32, (1, c_token), 1) // head_dim
    key_ok = lax.broadcasted_iota(jnp.int32, (1, LANES), 1) + (n_tok - LANES) < n_valid
    scale = head_dim ** -0.5 * LOG2E

    def block(k, b):
        r = k * n_blocks + b
        wq = lambda i: wqkvg_ref[b, :, i * c_token:(i + 1) * c_token]
        y = y_s[r, me]
        q = dot(y, wq(0)).astype(BF16)
        g = sigmoid(dot(y, wq(3)))
        q_heads = jnp.concatenate([jnp.where(lane == h, q, jnp.zeros_like(q)) for h in range(n_heads)], axis=0)
        for copy in copies(r):
            copy.wait_recv()
        y_all = y_s[r].reshape(n_tok, c_token)
        keys = dot(y_all, wq(1)).astype(BF16)
        values = dot(y_all, wq(2)).astype(BF16)
        scores = dot_t(q_heads, keys)
        probs = []
        for h in range(n_heads):
            sc = scores[h * tok_rows:(h + 1) * tok_rows] * scale + bias_s[b * n_heads + h]
            sc = jnp.concatenate([sc[:, :n_tok - LANES], jnp.where(key_ok, sc[:, n_tok - LANES:], MASK_VALUE * LOG2E)], axis=1)
            e = jnp.exp2(sc - jnp.max(sc, axis=1, keepdims=True))
            probs.append((e * (1.0 / jnp.sum(e, axis=1, keepdims=True))).astype(BF16))
        mixed = dot(jnp.concatenate(probs, axis=0), values)
        mix = mixed[:tok_rows]
        for h in range(1, n_heads):
            mix = jnp.where(lane == h, mixed[h * tok_rows:(h + 1) * tok_rows], mix)
        attn = dot((g * mix).astype(BF16), wao_ref[b])
        acts = acts_s[...] + gate_s[k, b, 2] * attn
        normed = (gate_s[k, b, 3] * norm_rows(acts) + gate_s[k, b, 4]).astype(BF16)
        h = dot(normed, wup_ref[b])
        half = h.shape[1] // 2
        act = (silu(h[:, :half]) * h[:, half:]).astype(BF16)
        acts_s[...] = acts + gate_s[k, b, 5] * dot(act, wdown_ref[b])
        for copy in copies(r):
            copy.wait_send()

    def step(k, carry):
        @pl.when(k > 0)
        def _():
            begin(k)
            send(k, 0, k * n_blocks)

        block(k, 0)
        for b in range(1, n_blocks):
            send(k, b, k * n_blocks + b)

            if b == 1:
                @pl.when(k == 0)
                def _():
                    for later in range(1, n_steps):
                        condition(later)

            block(k, b)
        xn, t, var = noisy(k)
        update = dot_t(wout_ref[...], norm_rows(acts_s[...]).astype(BF16))
        denoised = (SIGMA_DATA * SIGMA_DATA / var) * xn + (t * SIGMA_DATA / jnp.sqrt(var)) * update
        xs_s[...] = xn + STEP_SCALE * (sig_ref[k + 1] - t) * (xn - denoised) / t
        return carry

    lax.fori_loop(0, n_steps, step, 0)
    out_ref[...] = xs_s[...]


def solution(mesh):
    part_axes = ("sample", "tok")
    n_peers = mesh.shape["tok"]

    def local_run(s_trunk, s_inputs, z_trunk, x_noise, step_noise, sigmas, relpos_table, w_pair_in, w_z_up, w_z_down, w_pair_bias, w_single, fourier_w, fourier_b, w_fourier, w_s_up, w_s_down, w_in, w_s_tok, w_cond, gate_bias, w_qkvg, w_attn_out, w_up, w_down, w_out):
        tok_rows, n_tok, c_pair = z_trunk.shape
        n_steps, _, n_dim = step_noise.shape
        n_blocks, _, n_heads = w_pair_bias.shape
        n_layers, _, width = w_z_up.shape
        c_token = w_qkvg.shape[1]
        clip = (relpos_table.shape[0] - 1) // 2
        tile = c_pair * SUB
        n_var = 2 * clip // SUB + LANES // SUB + 2
        n_rounds = n_steps * n_blocks
        swap = lambda a: jnp.swapaxes(a, -1, -2)
        ops = [
            sigmas, swap(z_trunk), swap(relpos_table), swap(w_pair_in), w_z_up, swap(w_z_down), swap(w_pair_bias),
            s_trunk, s_inputs, swap(x_noise), swap(step_noise), w_single, fourier_w[None, :], fourier_b[None, :], w_fourier, w_s_up, w_s_down,
            w_in, w_s_tok, w_cond, gate_bias, w_qkvg, w_attn_out, w_up, w_down, swap(w_out),
        ]
        specs = [pl.BlockSpec(memory_space=pltpu.SMEM), pl.BlockSpec(memory_space=pl.ANY)] + [pl.BlockSpec(memory_space=pltpu.VMEM)] * (len(ops) - 2)
        out = pl.pallas_call(
            functools.partial(kernel, "tok", n_peers),
            in_specs=specs,
            out_specs=pl.BlockSpec(memory_space=pltpu.VMEM),
            out_shape=jax.ShapeDtypeStruct((n_dim, tok_rows), F32),
            scratch_shapes=[
                pltpu.VMEM((tok_rows, c_pair, n_tok), BF16),
                pltpu.VMEM((n_blocks * n_heads, tok_rows, n_tok), F32),
                pltpu.VMEM((tile, 2 * tile), BF16),
                pltpu.VMEM((n_layers, width * SUB, tile), BF16),
                pltpu.VMEM((n_layers, tile, width // 2 * SUB), BF16),
                pltpu.VMEM((n_blocks * n_heads * SUB, tile), BF16),
                pltpu.VMEM((tile, tile), BF16),
                pltpu.VMEM((n_var, tile, LANES), F32),
                pltpu.VMEM((n_var, SUB, LANES), F32),
                pltpu.VMEM((tile, CHUNK), F32),
                pltpu.VMEM((n_layers + 1, tile, CHUNK), F32),
                pltpu.VMEM((n_layers, tile, CHUNK), F32),
                pltpu.VMEM((n_layers, width // 2 * SUB, CHUNK), BF16),
                pltpu.VMEM((tok_rows, c_token), F32),
                pltpu.VMEM((SUB, c_token), F32),
                pltpu.VMEM((n_steps, tok_rows, c_token), F32),
                pltpu.VMEM((n_steps, n_blocks, 6, tok_rows, c_token), F32),
                pltpu.VMEM((tok_rows, c_token), F32),
                pltpu.VMEM((n_dim, tok_rows), F32),
                pltpu.VMEM((n_rounds, n_peers, tok_rows, c_token), BF16),
                pltpu.SemaphoreType.DMA,
                pltpu.SemaphoreType.DMA((n_rounds, n_peers - 1)),
                pltpu.SemaphoreType.DMA((n_rounds, n_peers - 1)),
            ],
            compiler_params=pltpu.CompilerParams(collective_id=0, has_side_effects=True, vmem_limit_bytes=60 * 1024 * 1024),
            name="sampler",
        )(*ops)
        return swap(out)

    in_specs = (P("tok", None), P("tok", None), P("tok", None, None), P(part_axes, None), P(None, part_axes, None)) + (P(),) * 21
    return jax.shard_map(local_run, mesh=mesh, in_specs=in_specs, out_specs=P(part_axes, None), check_vma=False)
```

time: 322 us -> 87 us (0.27)
  blocking collectives: 138 us -> 0 us
  matrix products: 88.8 us -> 0 us
  Pallas kernels: 0 us -> 85 us
  local copies, waits for them, and re-layouts: 42.9 us -> 1.26 us
  other arithmetic: 21.1 us -> 0 us
  between operations: 16.8 us -> 0.01 us
  loops' own time: 12.8 us -> 0 us
    all_gather x6 -> x0, blocking collectives: 138 us -> none  [local_run(): kv_all = lax.all_gather(kv_local, 'tok', axis=0, tiled=True)]
    pallas_call x0 -> x1, Pallas kernels: none -> 85 us  [local_run(): pl.pallas_call(functools.partial(kernel, 'tok', n_peers), in_specs=specs,...]
    dot_general x170 -> x0, matrix products: 75.8 us -> none  [the longest x38 17.8 us: transition(): jnp.dot(layer_norm(values).astype(jnp.bfloat16), w_up_one, preferred_elem...]
    dynamic_slice x32 -> x0, local copies, waits for them, and re-layouts: 25.7 us -> none  [the longest x16 15.6 us: one_group(): lax.dynamic_slice_in_dim(z_rows, group_idx * row_group, row_group, axis=0)]
    reduce_sum x111 -> x0, other arithmetic: 17.4 us -> none  [the longest x90 12.5 us: layer_norm(): variance = jnp.mean(centered * centered, axis=-1, keepdims=True)]
    sub x6 -> x0, matrix products: 13 us -> none  [local_run(): attn_probs = jax.nn.softmax(scores, axis=-1).astype(jnp.bfloat16)]
    another operation x1 -> x0, loops' own time: 12.8 us -> none  [pair_bias_rows(): groups = lax.map(one_group, jnp.arange(tok_rows // row_group))]
    dynamic_update_slice x16 -> x0, local copies, waits for them, and re-layouts: 12 us -> none  [pair_bias_rows(): groups = lax.map(one_group, jnp.arange(tok_rows // row_group))]
where the time goes in v2:
time: 87 us; the launch traced here: 86.3 us
  Pallas kernels  85 us (98%)
  local copies, waits for them, and re-layouts  1.26 us (1%)
    pallas_call x1, Pallas kernels, local_run(): pl.pallas_call(functools.partial(kernel, 'tok', n_peers), in_specs=specs,...  85 us

profile of v2, /device:TPU:112, one launch (start us, length us, event | category | flops | bytes accessed | tf_op | source)
XLA Modules:
  0.0 86.3 jit_solution(14573548437319259095)
XLA Ops:
  0.0 85.0 %sampler.1 = f32[3,128]{1,0:T(4,128)} custom-call(f32[4]{0:T(128)} %sig_ref.1, bf16[128,16,1024]{2,1,0:T(8,128)(2,1)} %bitcast.11, bf16[16,65]{1,0:T(8,128)(2,1)} %bitcast.15, bf16[16,32]{1,0:T(8,128)(2,1)} %bitcast.16, bf16[2,16,64]{2,1,0:T(8,128)(2,1)} %zup_ref.1, bf16[2,16,32]{2,1,0:T(8,128)(2,1)} %bitcast.13, bf16[2,4,16]{2,1,0:T(4,128)(2,1)} %bitcast.17, ...), custom_call_target="tpu_custom_call" | custom-call | tf_op jit(solution)/shard_map/sampler/pallas_call | solution.py:351
  85.0 1.3 %copy.28 = f32[128,3]{0,1:T(4,128)} copy(f32[128,3]{0,1:T(4,128)} %bitcast.12) | data formatting | bytes 3072

commit v3 on v2

--- a/solution.py
+++ b/solution.py
@@ -17,6 +17,7 @@
 LANES = 128
 SUB = 8
 CHUNK = 256
+UNROLL = 7
 F32 = jnp.float32
 BF16 = jnp.bfloat16
 
@@ -77,7 +78,7 @@
     win_ref, wstok_ref, wcond_ref, gbias_ref, wqkvg_ref, wao_ref, wup_ref, wdown_ref, wout_ref,
     out_ref,
     z_s, bias_s, pwin_s, pwup_s, pwdown_s, pwpb_s, perm_s, rel_s, relsum_s,
-    zp_s, cond_ss, held_ss, act_ss,
+    zn_s, xn_ss, cond_ss, held_ss, act_ss,
     base_s, four_s, astok_s, gate_s, acts_s, xs_s, y_s,
     z_sem, send_sem, recv_sem,
 ):
@@ -132,7 +133,7 @@
 
     def copies(r):
         out = []
-        for off in range(1, n_peers):
+        for off in sorted(range(1, n_peers), key=lambda o: -min(o, n_peers - o)):
             peer = lax.rem(me + off, n_peers)
             out.append(pltpu.make_async_remote_copy(
                 src_ref=y_s.at[r, me], dst_ref=y_s.at[r, me],
@@ -217,51 +218,70 @@
     total = (tok_rows // SUB) * n_chunks
     depth = 2 + 2 * n_layers
 
-    def place(it, lag):
-        idx = jnp.clip(it - lag, 0, total - 1)
-        return (idx // n_chunks) * SUB, (idx % n_chunks) * CHUNK
-
-    def trip(it, carry):
-        r0, c0 = place(it, depth)
-        bias = dot(pwpb_s[...], norm_major(cond_ss[n_layers]))
-        bias = bias.astype(BF16).astype(F32) * LOG2E
-        bias_s[:, pl.ds(pl.multiple_of(r0, SUB), SUB), pl.ds(pl.multiple_of(c0, CHUNK), CHUNK)] = bias.reshape(n_blocks * n_heads, SUB, CHUNK)
+    def trip(it):
+        known = isinstance(it, int)
+
+        def active(lag):
+            return not known or 0 <= it - lag < total
+
+        def place(lag):
+            idx = it - lag
+            r0, c0 = (idx // n_chunks) * SUB, (idx % n_chunks) * CHUNK
+            return (r0, c0) if known else (pl.multiple_of(r0, SUB), pl.multiple_of(c0, CHUNK))
+
+        if active(depth):
+            r0, c0 = place(depth)
+            bias = dot(pwpb_s[...], xn_ss[n_layers])
+            bias = bias.astype(BF16).astype(F32) * LOG2E
+            bias_s[:, pl.ds(r0, SUB), pl.ds(c0, CHUNK)] = bias.reshape(n_blocks * n_heads, SUB, CHUNK)
         for layer in reversed(range(n_layers)):
-            cond_ss[layer + 1] = held_ss[layer] + dot(pwdown_s[layer], act_ss[layer])
-            cond = cond_ss[layer]
-            h = dot(pwup_s[layer], norm_major(cond))
-            half = h.shape[0] // 2
-            gate = h[:half]
-            act_ss[layer] = ((gate + gate * jnp.tanh(gate)) * h[half:]).astype(BF16)
-            held_ss[layer] = cond
-        r0, c0 = place(it, 1)
-        z = zp_s[...].reshape(c_pair, SUB, CHUNK)
-        rels, sums = [], []
-        for part in range(CHUNK // LANES):
-            delta = me * tok_rows + r0 - c0 - part * LANES
-            v = jnp.clip(delta // SUB + low, 0, n_var - 1)
-            rels.append(rel_s[v])
-            sums.append(relsum_s[v])
-        rel = jnp.concatenate(rels, axis=1).reshape(c_pair, SUB, CHUNK)
-        inv = 1.0 / (2 * c_pair)
-        mean = (jnp.sum(z, axis=0) + jnp.concatenate(sums, axis=1)) * inv
-        zc = z - mean
-        rc = rel - mean
-        var = (jnp.sum(zc * zc, axis=0) + jnp.sum(rc * rc, axis=0)) * inv
-        rs = lax.rsqrt(var + EPS)
-        zn = (zc * rs).reshape(tile, CHUNK).astype(BF16)
-        rn = (rc * rs).reshape(tile, CHUNK).astype(BF16)
-        cond_ss[0] = dot(pwin_s[...], jnp.concatenate([zn, rn], axis=0))
-        r0, c0 = place(it, 0)
-        zb = z_s[pl.ds(r0, SUB), :, pl.ds(pl.multiple_of(c0, CHUNK), CHUNK)].reshape(tile, CHUNK)
-        zp_s[...] = dot(perm_s[...], zb)
+            if active(3 + 2 * layer):
+                cond = held_ss[layer] + dot(pwdown_s[layer], act_ss[layer])
+                xn_ss[layer + 1] = norm_major(cond)
+            if active(2 + 2 * layer):
+                h = dot(pwup_s[layer], xn_ss[layer])
+                half = h.shape[0] // 2
+                gate = h[:half]
+                act_ss[layer] = ((gate + gate * jnp.tanh(gate)) * h[half:]).astype(BF16)
+                held_ss[layer] = cond_ss[layer]
+            if active(3 + 2 * layer) and layer + 1 < n_layers:
+                cond_ss[layer + 1] = cond
+        if active(1):
+            cond = dot(pwin_s[...], zn_s[...])
+            cond_ss[0] = cond
+            xn_ss[0] = norm_major(cond)
+        if active(0):
+            r0, c0 = place(0)
+            zb = z_s[pl.ds(r0, SUB), :, pl.ds(c0, CHUNK)].reshape(tile, CHUNK)
+            z = dot(perm_s[...], zb).reshape(c_pair, SUB, CHUNK)
+            rels, sums = [], []
+            for part in range(CHUNK // LANES):
+                delta = me * tok_rows + r0 - c0 - part * LANES
+                v = jnp.clip(delta // SUB + low, 0, n_var - 1)
+                rels.append(rel_s[v])
+                sums.append(relsum_s[v])
+            rel = jnp.concatenate(rels, axis=1).reshape(c_pair, SUB, CHUNK)
+            inv = 1.0 / (2 * c_pair)
+            mean = (jnp.sum(z, axis=0) + jnp.concatenate(sums, axis=1)) * inv
+            zc = z - mean
+            rc = rel - mean
+            var = (jnp.sum(zc * zc, axis=0) + jnp.sum(rc * rc, axis=0)) * inv
+            rs = lax.rsqrt(var + EPS)
+            zn_s[:tile] = (zc * rs).reshape(tile, CHUNK).astype(BF16)
+            zn_s[tile:] = (rc * rs).reshape(tile, CHUNK).astype(BF16)
+
+    loops = (total - depth) // UNROLL
+
+    def trips(i, carry):
+        for j in range(UNROLL):
+            trip(depth + i * UNROLL + j)
         return carry
 
-    zp_s[...] = jnp.zeros(zp_s.shape, F32)
-    cond_ss[...] = jnp.zeros(cond_ss.shape, F32)
-    held_ss[...] = jnp.zeros(held_ss.shape, F32)
-    act_ss[...] = jnp.zeros(act_ss.shape, BF16)
-    lax.fori_loop(0, total + depth, trip, 0)
+    for it in range(depth):
+        trip(it)
+    lax.fori_loop(0, loops, trips, 0)
+    for it in range(depth + loops * UNROLL, total + depth):
+        trip(it)
 
     lane = lax.broadcasted_iota(jnp.int32, (1, c_token), 1) // head_dim
     key_ok = lax.broadcasted_iota(jnp.int32, (1, LANES), 1) + (n_tok - LANES) < n_valid
@@ -363,8 +383,9 @@
                 pltpu.VMEM((tile, tile), BF16),
                 pltpu.VMEM((n_var, tile, LANES), F32),
                 pltpu.VMEM((n_var, SUB, LANES), F32),
-                pltpu.VMEM((tile, CHUNK), F32),
-                pltpu.VMEM((n_layers + 1, tile, CHUNK), F32),
+                pltpu.VMEM((2 * tile, CHUNK), BF16),
+                pltpu.VMEM((n_layers + 1, tile, CHUNK), BF16),
+                pltpu.VMEM((n_layers, tile, CHUNK), F32),
                 pltpu.VMEM((n_layers, tile, CHUNK), F32),
                 pltpu.VMEM((n_layers, width // 2 * SUB, CHUNK), BF16),
                 pltpu.VMEM((tok_rows, c_token), F32),

time: 87 us -> 76.8 us (0.88)
  Pallas kernels: 85 us -> 75.4 us
    pallas_call x1, Pallas kernels: 85 us -> 75.4 us  [local_run(): pl.pallas_call(functools.partial(kernel, 'tok', n_peers), in_specs=specs,...]
where the time goes in v3:
time: 76.8 us; the launch traced here: 76.7 us
  Pallas kernels  75.4 us (98%)
  local copies, waits for them, and re-layouts  1.26 us (2%)
    pallas_call x1, Pallas kernels, local_run(): pl.pallas_call(functools.partial(kernel, 'tok', n_peers), in_specs=specs,...  75.4 us

profile of v3, /device:TPU:112, one launch (start us, length us, event | category | flops | bytes accessed | tf_op | source)
XLA Modules:
  0.0 76.7 jit_solution(14882918142175369961)
XLA Ops:
  0.0 75.4 %sampler.1 = f32[3,128]{1,0:T(4,128)} custom-call(f32[4]{0:T(128)} %sig_ref.1, bf16[128,16,1024]{2,1,0:T(8,128)(2,1)} %bitcast.11, bf16[16,65]{1,0:T(8,128)(2,1)} %bitcast.15, bf16[16,32]{1,0:T(8,128)(2,1)} %bitcast.16, bf16[2,16,64]{2,1,0:T(8,128)(2,1)} %zup_ref.1, bf16[2,16,32]{2,1,0:T(8,128)(2,1)} %bitcast.13, bf16[2,4,16]{2,1,0:T(4,128)(2,1)} %bitcast.17, ...), custom_call_target="tpu_custom_call" | custom-call | tf_op jit(solution)/shard_map/sampler/pallas_call | solution.py:371
  75.4 1.3 %copy.28 = f32[128,3]{0,1:T(4,128)} copy(f32[128,3]{0,1:T(4,128)} %bitcast.12) | data formatting | bytes 3072

commit v4 on v3

--- a/solution.py
+++ b/solution.py
@@ -18,6 +18,7 @@
 SUB = 8
 CHUNK = 256
 UNROLL = 7
+GROUPS = ((0,), (2, 1, 3))
 F32 = jnp.float32
 BF16 = jnp.bfloat16
 
@@ -53,6 +54,17 @@
     centered = parts - jnp.sum(parts, axis=0, keepdims=True) * inv
     variance = jnp.sum(centered * centered, axis=0, keepdims=True) * inv
     return (centered * lax.rsqrt(variance + EPS)).reshape(values.shape).astype(BF16)
+
+
+def dot_tn(a, b):
+    return lax.dot_general(a, b, (((0,), (0,)), ((), ())), preferred_element_type=F32)
+
+
+def norm_cols(values):
+    inv = 1.0 / values.shape[0]
+    centered = values - jnp.sum(values, axis=0, keepdims=True) * inv
+    variance = jnp.sum(centered * centered, axis=0, keepdims=True) * inv
+    return centered * lax.rsqrt(variance + EPS)
 
 
 def norm_rows(values):
@@ -79,6 +91,7 @@
     out_ref,
     z_s, bias_s, pwin_s, pwup_s, pwdown_s, pwpb_s, perm_s, rel_s, relsum_s,
     zn_s, xn_ss, cond_ss, held_ss, act_ss,
+    bias_ts, wqkvg_ts, wao_ts, wup_ts, wdown_ts, cols_s, win_s, e_s, vt_s,
     base_s, four_s, astok_s, gate_s, acts_s, xs_s, y_s,
     z_sem, send_sem, recv_sem,
 ):
@@ -96,8 +109,11 @@
     n_var = rel_s.shape[0]
     low = (clip + SUB) // SUB
 
-    z_copy = pltpu.make_async_copy(z_hbm, z_s, z_sem)
-    z_copy.start()
+    first = SUB * pl.cdiv(2 + 2 * n_layers, n_tok // CHUNK)
+    z_parts = [pl.ds(0, first), pl.ds(first, tok_rows - first)]
+    z_copies = [pltpu.make_async_copy(z_hbm.at[part], z_s.at[part], z_sem.at[i]) for i, part in enumerate(z_parts)]
+    for copy in z_copies:
+        copy.start()
     barrier = pltpu.get_barrier_semaphore()
     for off in range(1, n_peers):
         pl.semaphore_signal(barrier, inc=1, device_id={axis: lax.rem(me + off, n_peers)}, device_id_type=pl.DeviceIdType.MESH)
@@ -108,28 +124,35 @@
         t_col = jnp.where(row == k, sig_ref[k] * (1.0 + GAMMA), t_col)
     level = 0.25 * jnp.log(t_col / SIGMA_DATA)
     feat = jnp.cos(2.0 * math.pi * (level * fw_ref[...] + fb_ref[...]))
-    four_s[...] = dot(norm_rows(feat).astype(BF16), wfour_ref[...])
+    four_s[...] = lax.dot_general(wfour_ref[...], norm_rows(feat).astype(BF16), (((0,), (1,)), ((), ())), preferred_element_type=F32)
     joined = norm_rows(jnp.concatenate([st_ref[...].astype(F32), si_ref[...].astype(F32)], axis=-1)).astype(BF16)
-    base_s[...] = dot(joined, wsingle_ref[...])
+    base_s[...] = lax.dot_general(wsingle_ref[...], joined, (((0,), (1,)), ((), ())), preferred_element_type=F32)
+    n_dim = x_ref.shape[0]
+    small = [gbias_ref[b] for b in range(n_blocks)] + [win_ref[...]]
+    n_small = 2 * n_blocks + n_dim
+    cols = jnp.transpose(jnp.concatenate(small + [jnp.zeros((-n_small % SUB, c_token), F32)], axis=0))
+    cols_s[...] = cols
+    for d in range(n_dim):
+        win_s[d] = jnp.broadcast_to(cols[:, 2 * n_blocks + d:2 * n_blocks + d + 1], (c_token, tok_rows))
 
     def condition(k):
-        single = base_s[...] + four_s[pl.ds(k, 1), :]
+        single = base_s[...] + four_s[:, k:k + 1]
         for layer in range(wsup_ref.shape[0]):
-            h = dot(norm_rows(single).astype(BF16), wsup_ref[layer])
-            half = h.shape[1] // 2
-            act = (silu(h[:, :half]) * h[:, half:]).astype(BF16)
-            single = single + dot(act, wsdown_ref[layer])
-        u = norm_rows(single).astype(BF16)
-        astok_s[k] = dot(u, wstok_ref[...])
+            h = dot_tn(wsup_ref[layer], norm_cols(single).astype(BF16))
+            half = h.shape[0] // 2
+            act = (silu(h[:half]) * h[half:]).astype(BF16)
+            single = single + dot_tn(wsdown_ref[layer], act)
+        u = norm_cols(single).astype(BF16)
+        astok_s[k] = dot_tn(wstok_ref[...], u)
         for b in range(n_blocks):
-            cond = dot(u, wcond_ref[b])
-            part = lambda i: cond[:, i * c_token:(i + 1) * c_token]
+            cond = dot_tn(wcond_ref[b], u)
+            part = lambda i: cond[i * c_token:(i + 1) * c_token]
             gate_s[k, b, 0] = sigmoid(part(0))
             gate_s[k, b, 1] = part(1)
-            gate_s[k, b, 2] = sigmoid(part(2) + gbias_ref[b, 0:1, :])
+            gate_s[k, b, 2] = sigmoid(part(2) + cols_s[:, 2 * b:2 * b + 1])
             gate_s[k, b, 3] = sigmoid(part(3))
             gate_s[k, b, 4] = part(4)
-            gate_s[k, b, 5] = sigmoid(part(5) + gbias_ref[b, 1:2, :])
+            gate_s[k, b, 5] = sigmoid(part(5) + cols_s[:, 2 * b + 1:2 * b + 2])
 
     def copies(r):
         out = []
@@ -137,9 +160,15 @@
             peer = lax.rem(me + off, n_peers)
             out.append(pltpu.make_async_remote_copy(
                 src_ref=y_s.at[r, me], dst_ref=y_s.at[r, me],
-                send_sem=send_sem.at[r, off - 1], recv_sem=recv_sem.at[r, off - 1],
+                send_sem=send_sem.at[r, off], recv_sem=recv_sem.at[r, me],
                 device_id={axis: peer}, device_id_type=pl.DeviceIdType.MESH))
         return out
+
+    def wait_from(r, src):
+        pltpu.make_async_remote_copy(
+            src_ref=y_s.at[r, src], dst_ref=y_s.at[r, src],
+            send_sem=send_sem.at[r, 0], recv_sem=recv_sem.at[r, src],
+            device_id={axis: src}, device_id_type=pl.DeviceIdType.MESH).wait_recv()
 
     def noisy(k):
         c = jnp.full((1, tok_rows), sig_ref[k], F32)
@@ -150,24 +179,17 @@
     def begin(k):
         xn, t, var = noisy(k)
         r = xn / jnp.sqrt(var)
-        cols = jnp.transpose(jnp.concatenate([r, jnp.zeros((SUB - r.shape[0], r.shape[1]), F32)], axis=0))
-        acts = astok_s[k]
-        lin = cols[:, 0:1] * win_ref[0:1, :]
-        for d in range(1, r.shape[0]):
-            lin = lin + cols[:, d:d + 1] * win_ref[d:d + 1, :]
-        acts_s[...] = lin + acts
-
-    def send(k, b, r):
-        y = (gate_s[k, b, 0] * norm_rows(acts_s[...]) + gate_s[k, b, 1]).astype(BF16)
-        y_s[r, me] = y
+        lin = r[0:1] * win_s[0]
+        for d in range(1, n_dim):
+            lin = lin + r[d:d + 1] * win_s[d]
+        acts_s[...] = lin + astok_s[k]
+
+    def pack(k, b, r):
+        y_s[r, me] = (gate_s[k, b, 0] * norm_cols(acts_s[...]) + gate_s[k, b, 1]).astype(BF16)
+
+    def send(r):
         for copy in copies(r):
             copy.start()
-
-    condition(0)
-    xs_s[...] = sig_ref[0] * x_ref[...]
-    begin(0)
-    pl.semaphore_wait(barrier, n_peers - 1)
-    send(0, 0, 0)
 
     pin = pin_ref[...]
     pwin_s[:, :tile] = expand(pin[:, :c_pair])
@@ -198,21 +220,16 @@
     k_i = lax.broadcasted_iota(jnp.int32, (LANES, LANES), 0)
     j_i = lax.broadcasted_iota(jnp.int32, (LANES, LANES), 1)
 
-    def fill(i, carry):
+    for i in range(0, n_var, per):
         picks = []
-        for p in range(per):
-            delta = SUB * (i * per + p - low)
-            want = jnp.clip(delta - j_i + clip + SUB - 1, 0, n_bins + SUB - 2)
+        for v in range(i, i + per):
+            want = jnp.clip(SUB * (v - low) - j_i + clip + SUB - 1, 0, n_bins + SUB - 2)
             picks.append((k_i == want).astype(BF16))
         planes = dot(tab, jnp.concatenate(picks, axis=1))
-        for p in range(per):
-            plane = planes[:, p * LANES:(p + 1) * LANES]
-            rel_s[i * per + p] = plane
-            relsum_s[i * per + p] = jnp.sum(plane.reshape(c_pair, SUB, LANES), axis=0)
-        return carry
-
-    lax.fori_loop(0, n_var // per, fill, 0)
-    z_copy.wait()
+        for v in range(i, i + per):
+            plane = planes[:, (v - i) * LANES:(v - i + 1) * LANES]
+            rel_s[v] = plane
+            relsum_s[v] = jnp.sum(plane.reshape(c_pair, SUB, LANES), axis=0)
 
     n_chunks = n_tok // CHUNK
     total = (tok_rows // SUB) * n_chunks
@@ -277,68 +294,110 @@
             trip(depth + i * UNROLL + j)
         return carry
 
+    for b in range(n_blocks):
+        wqkvg_ts[b] = jnp.transpose(wqkvg_ref[b])
+        wao_ts[b] = jnp.transpose(wao_ref[b])
+        wup_ts[b] = jnp.transpose(wup_ref[b])
+        wdown_ts[b] = jnp.transpose(wdown_ref[b])
+    z_copies[0].wait()
+    condition(0)
+    xs_s[...] = sig_ref[0] * x_ref[...]
+    begin(0)
     for it in range(depth):
         trip(it)
+    pack(0, 0, 0)
+    pl.semaphore_wait(barrier, n_peers - 1)
+    send(0)
+    z_copies[1].wait()
     lax.fori_loop(0, loops, trips, 0)
     for it in range(depth + loops * UNROLL, total + depth):
         trip(it)
 
-    lane = lax.broadcasted_iota(jnp.int32, (1, c_token), 1) // head_dim
-    key_ok = lax.broadcasted_iota(jnp.int32, (1, LANES), 1) + (n_tok - LANES) < n_valid
+    def turn(b):
+        for h in range(n_heads):
+            for key0 in range(0, n_tok, LANES):
+                bias_ts[b, key0:key0 + LANES, h * tok_rows:(h + 1) * tok_rows] = jnp.transpose(bias_s[b * n_heads + h, :, key0:key0 + LANES])
+
+    head = lax.broadcasted_iota(jnp.int32, (c_token, 1), 0) // head_dim
     scale = head_dim ** -0.5 * LOG2E
+    cores = 2
+    n_chips = n_peers // cores
+    chip_keys = cores * tok_rows
+    my_chip = me // cores
 
     def block(k, b):
         r = k * n_blocks + b
-        wq = lambda i: wqkvg_ref[b, :, i * c_token:(i + 1) * c_token]
         y = y_s[r, me]
-        q = dot(y, wq(0)).astype(BF16)
-        g = sigmoid(dot(y, wq(3)))
-        q_heads = jnp.concatenate([jnp.where(lane == h, q, jnp.zeros_like(q)) for h in range(n_heads)], axis=0)
-        for copy in copies(r):
-            copy.wait_recv()
-        y_all = y_s[r].reshape(n_tok, c_token)
-        keys = dot(y_all, wq(1)).astype(BF16)
-        values = dot(y_all, wq(2)).astype(BF16)
-        scores = dot_t(q_heads, keys)
-        probs = []
-        for h in range(n_heads):
-            sc = scores[h * tok_rows:(h + 1) * tok_rows] * scale + bias_s[b * n_heads + h]
-            sc = jnp.concatenate([sc[:, :n_tok - LANES], jnp.where(key_ok, sc[:, n_tok - LANES:], MASK_VALUE * LOG2E)], axis=1)
-            e = jnp.exp2(sc - jnp.max(sc, axis=1, keepdims=True))
-            probs.append((e * (1.0 / jnp.sum(e, axis=1, keepdims=True))).astype(BF16))
-        mixed = dot(jnp.concatenate(probs, axis=0), values)
-        mix = mixed[:tok_rows]
-        for h in range(1, n_heads):
-            mix = jnp.where(lane == h, mixed[h * tok_rows:(h + 1) * tok_rows], mix)
-        attn = dot((g * mix).astype(BF16), wao_ref[b])
+        q = dot(wqkvg_ts[b, :c_token, :], y)
+        g = sigmoid(dot(wqkvg_ts[b, 3 * c_token:, :], y))
+        q_heads = jnp.concatenate([jnp.where(head == h, q, 0.0).astype(BF16) for h in range(n_heads)], axis=1)
+        tops, sums = [], []
+        pos = 0
+        for group in GROUPS:
+            chips = [lax.rem(my_chip + d, n_chips) for d in group]
+            for d, chip in zip(group, chips):
+                if d == 0:
+                    wait_from(r, me + 1 - 2 * lax.rem(me, cores))
+                else:
+                    for c in range(cores):
+                        wait_from(r, chip * cores + c)
+            y_group = jnp.concatenate([y_s[r, chip * cores + c] for chip in chips for c in range(cores)], axis=1)
+            kv = dot(wqkvg_ts[b, c_token:3 * c_token, :], y_group).astype(BF16)
+            vt_s[:, pos * chip_keys:(pos + len(group)) * chip_keys] = kv[c_token:]
+            scores = dot_tn(kv[:c_token], q_heads)
+            for i, chip in enumerate(chips):
+                key0 = pl.multiple_of(chip * chip_keys, chip_keys)
+                sc = scores[i * chip_keys:(i + 1) * chip_keys] * scale + bias_ts[b, pl.ds(key0, chip_keys), :]
+                key_ok = lax.broadcasted_iota(jnp.int32, (chip_keys, 1), 0) + key0 < n_valid
+                sc = jnp.where(key_ok, sc, MASK_VALUE * LOG2E)
+                top = jnp.max(sc, axis=0, keepdims=True)
+                e = jnp.exp2(sc - top)
+                e_s[pos] = e
+                tops.append(top)
+                sums.append(jnp.sum(e, axis=0, keepdims=True))
+                pos += 1
+        best = functools.reduce(jnp.maximum, tops)
+        scales = [jnp.exp2(top - best) for top in tops]
+        inv = 1.0 / functools.reduce(jnp.add, [f * l for f, l in zip(scales, sums)])
+        probs = jnp.concatenate([(e_s[i] * (scales[i] * inv)).astype(BF16) for i in range(pos)], axis=0)
+        mix = []
+        for h in range(0, n_heads, 2):
+            pair = dot(vt_s[h * head_dim:(h + 2) * head_dim, :], probs[:, h * tok_rows:(h + 2) * tok_rows])
+            mix += [pair[:head_dim, :tok_rows], pair[head_dim:, tok_rows:]]
+        attn = dot(wao_ts[b], (g * jnp.concatenate(mix, axis=0)).astype(BF16))
         acts = acts_s[...] + gate_s[k, b, 2] * attn
-        normed = (gate_s[k, b, 3] * norm_rows(acts) + gate_s[k, b, 4]).astype(BF16)
-        h = dot(normed, wup_ref[b])
-        half = h.shape[1] // 2
-        act = (silu(h[:, :half]) * h[:, half:]).astype(BF16)
-        acts_s[...] = acts + gate_s[k, b, 5] * dot(act, wdown_ref[b])
+        normed = (gate_s[k, b, 3] * norm_cols(acts) + gate_s[k, b, 4]).astype(BF16)
+        h = dot(wup_ts[b], normed)
+        half = h.shape[0] // 2
+        act = (silu(h[:half]) * h[half:]).astype(BF16)
+        acts_s[...] = acts + gate_s[k, b, 5] * dot(wdown_ts[b], act)
         for copy in copies(r):
             copy.wait_send()
+
+    turn(0)
 
     def step(k, carry):
         @pl.when(k > 0)
         def _():
             begin(k)
-            send(k, 0, k * n_blocks)
+            pack(k, 0, k * n_blocks)
+            send(k * n_blocks)
 
         block(k, 0)
         for b in range(1, n_blocks):
-            send(k, b, k * n_blocks + b)
-
-            if b == 1:
-                @pl.when(k == 0)
-                def _():
+            pack(k, b, k * n_blocks + b)
+            send(k * n_blocks + b)
+
+            @pl.when(k == 0)
+            def _():
+                turn(b)
+                if b == 1:
                     for later in range(1, n_steps):
                         condition(later)
 
             block(k, b)
         xn, t, var = noisy(k)
-        update = dot_t(wout_ref[...], norm_rows(acts_s[...]).astype(BF16))
+        update = dot(wout_ref[...], norm_cols(acts_s[...]).astype(BF16))
         denoised = (SIGMA_DATA * SIGMA_DATA / var) * xn + (t * SIGMA_DATA / jnp.sqrt(var)) * update
         xs_s[...] = xn + STEP_SCALE * (sig_ref[k + 1] - t) * (xn - denoised) / t
         return carry
@@ -388,16 +447,25 @@
                 pltpu.VMEM((n_layers, tile, CHUNK), F32),
                 pltpu.VMEM((n_layers, tile, CHUNK), F32),
                 pltpu.VMEM((n_layers, width // 2 * SUB, CHUNK), BF16),
-                pltpu.VMEM((tok_rows, c_token), F32),
-                pltpu.VMEM((SUB, c_token), F32),
-                pltpu.VMEM((n_steps, tok_rows, c_token), F32),
-                pltpu.VMEM((n_steps, n_blocks, 6, tok_rows, c_token), F32),
-                pltpu.VMEM((tok_rows, c_token), F32),
+                pltpu.VMEM((n_blocks, n_tok, n_heads * tok_rows), F32),
+                pltpu.VMEM((n_blocks, 4 * c_token, c_token), BF16),
+                pltpu.VMEM((n_blocks, c_token, c_token), BF16),
+                pltpu.VMEM((n_blocks, w_up.shape[2], c_token), BF16),
+                pltpu.VMEM((n_blocks, c_token, w_down.shape[1]), BF16),
+                pltpu.VMEM((c_token, SUB), F32),
+                pltpu.VMEM((n_dim, c_token, tok_rows), F32),
+                pltpu.VMEM((n_peers // 2, 2 * tok_rows, n_heads * tok_rows), F32),
+                pltpu.VMEM((c_token, n_tok), BF16),
+                pltpu.VMEM((c_token, tok_rows), F32),
+                pltpu.VMEM((c_token, SUB), F32),
+                pltpu.VMEM((n_steps, c_token, tok_rows), F32),
+                pltpu.VMEM((n_steps, n_blocks, 6, c_token, tok_rows), F32),
+                pltpu.VMEM((c_token, tok_rows), F32),
                 pltpu.VMEM((n_dim, tok_rows), F32),
-                pltpu.VMEM((n_rounds, n_peers, tok_rows, c_token), BF16),
-                pltpu.SemaphoreType.DMA,
-                pltpu.SemaphoreType.DMA((n_rounds, n_peers - 1)),
-                pltpu.SemaphoreType.DMA((n_rounds, n_peers - 1)),
+                pltpu.VMEM((n_rounds, n_peers, c_token, tok_rows), BF16),
+                pltpu.SemaphoreType.DMA((2,)),
+                pltpu.SemaphoreType.DMA((n_rounds, n_peers)),
+                pltpu.SemaphoreType.DMA((n_rounds, n_peers)),
             ],
             compiler_params=pltpu.CompilerParams(collective_id=0, has_side_effects=True, vmem_limit_bytes=60 * 1024 * 1024),
             name="sampler",

time: 76.8 us -> 70.8 us (0.922)
  Pallas kernels: 75.4 us -> 69.4 us
    pallas_call x1, Pallas kernels: 75.4 us -> 69.4 us  [local_run(): pl.pallas_call(functools.partial(kernel, 'tok', n_peers), in_specs=specs,...]
where the time goes in v4:
time: 70.8 us; the launch traced here: 70.7 us
  Pallas kernels  69.4 us (98%)
  local copies, waits for them, and re-layouts  1.26 us (2%)
    pallas_call x1, Pallas kernels, local_run(): pl.pallas_call(functools.partial(kernel, 'tok', n_peers), in_specs=specs,...  69.4 us

profile of v4, /device:TPU:112, one launch (start us, length us, event | category | flops | bytes accessed | tf_op | source)
XLA Modules:
  0.0 70.7 jit_solution(5340786790213796838)
XLA Ops:
  0.0 69.4 %sampler.1 = f32[3,128]{1,0:T(4,128)} custom-call(f32[4]{0:T(128)} %sig_ref.1, bf16[128,16,1024]{2,1,0:T(8,128)(2,1)} %bitcast.11, bf16[16,65]{1,0:T(8,128)(2,1)} %bitcast.15, bf16[16,32]{1,0:T(8,128)(2,1)} %bitcast.16, bf16[2,16,64]{2,1,0:T(8,128)(2,1)} %zup_ref.1, bf16[2,16,32]{2,1,0:T(8,128)(2,1)} %bitcast.13, bf16[2,4,16]{2,1,0:T(4,128)(2,1)} %bitcast.17, ...), custom_call_target="tpu_custom_call" | custom-call | tf_op jit(solution)/shard_map/sampler/pallas_call | solution.py:430
  69.4 1.3 %copy.28 = f32[128,3]{0,1:T(4,128)} copy(f32[128,3]{0,1:T(4,128)} %bitcast.12) | data formatting | bytes 3072

commit v5 on v4

--- a/solution.py
+++ b/solution.py
@@ -92,8 +92,8 @@
     z_s, bias_s, pwin_s, pwup_s, pwdown_s, pwpb_s, perm_s, rel_s, relsum_s,
     zn_s, xn_ss, cond_ss, held_ss, act_ss,
     bias_ts, wqkvg_ts, wao_ts, wup_ts, wdown_ts, cols_s, win_s, e_s, vt_s,
-    base_s, four_s, astok_s, gate_s, acts_s, xs_s, y_s,
-    z_sem, send_sem, recv_sem,
+    base_s, four_s, astok_s, gate_s, acts_s, xs_s, y_s, u_own, u_s, r_s, ast_all, mul_all, add_all,
+    z_sem, y_send, y_recv, u_send, u_recv, r_send, r_recv,
 ):
     me = lax.axis_index(axis)
     tok_rows, c_pair, n_tok = z_hbm.shape
@@ -135,40 +135,50 @@
     for d in range(n_dim):
         win_s[d] = jnp.broadcast_to(cols[:, 2 * n_blocks + d:2 * n_blocks + d + 1], (c_token, tok_rows))
 
-    def condition(k):
-        single = base_s[...] + four_s[:, k:k + 1]
+    def condition():
+        single = jnp.concatenate([base_s[...] + four_s[:, k:k + 1] for k in range(n_steps)], axis=1)
         for layer in range(wsup_ref.shape[0]):
             h = dot_tn(wsup_ref[layer], norm_cols(single).astype(BF16))
             half = h.shape[0] // 2
             act = (silu(h[:half]) * h[half:]).astype(BF16)
             single = single + dot_tn(wsdown_ref[layer], act)
         u = norm_cols(single).astype(BF16)
-        astok_s[k] = dot_tn(wstok_ref[...], u)
+        for k in range(n_steps):
+            u_own[k] = u[:, k * tok_rows:(k + 1) * tok_rows]
+
+    def gates(first, last):
+        u = jnp.concatenate([u_own[k] for k in range(first, last)], axis=1)
+        acts = dot_tn(wstok_ref[...], u)
+        at = lambda v, k: v[:, (k - first) * tok_rows:(k - first + 1) * tok_rows]
+        for k in range(first, last):
+            astok_s[k] = at(acts, k)
         for b in range(n_blocks):
             cond = dot_tn(wcond_ref[b], u)
             part = lambda i: cond[i * c_token:(i + 1) * c_token]
-            gate_s[k, b, 0] = sigmoid(part(0))
-            gate_s[k, b, 1] = part(1)
-            gate_s[k, b, 2] = sigmoid(part(2) + cols_s[:, 2 * b:2 * b + 1])
-            gate_s[k, b, 3] = sigmoid(part(3))
-            gate_s[k, b, 4] = part(4)
-            gate_s[k, b, 5] = sigmoid(part(5) + cols_s[:, 2 * b + 1:2 * b + 2])
-
-    def copies(r):
+            rows = [sigmoid(part(0)), part(1), sigmoid(part(2) + cols_s[:, 2 * b:2 * b + 1]), sigmoid(part(3)), part(4), sigmoid(part(5) + cols_s[:, 2 * b + 1:2 * b + 2])]
+            for i, gate in enumerate(rows):
+                for k in range(first, last):
+                    gate_s[k, b, i] = at(gate, k)
+
+    def copies(buf, i, send_sem, recv_sem):
         out = []
         for off in sorted(range(1, n_peers), key=lambda o: -min(o, n_peers - o)):
             peer = lax.rem(me + off, n_peers)
             out.append(pltpu.make_async_remote_copy(
-                src_ref=y_s.at[r, me], dst_ref=y_s.at[r, me],
-                send_sem=send_sem.at[r, off], recv_sem=recv_sem.at[r, me],
+                src_ref=buf.at[i, me], dst_ref=buf.at[i, me],
+                send_sem=send_sem.at[i, off], recv_sem=recv_sem.at[i, me],
                 device_id={axis: peer}, device_id_type=pl.DeviceIdType.MESH))
         return out
 
-    def wait_from(r, src):
+    def wait_from(buf, i, send_sem, recv_sem, src):
         pltpu.make_async_remote_copy(
-            src_ref=y_s.at[r, src], dst_ref=y_s.at[r, src],
-            send_sem=send_sem.at[r, 0], recv_sem=recv_sem.at[r, src],
+            src_ref=buf.at[i, src], dst_ref=buf.at[i, src],
+            send_sem=send_sem.at[i, 0], recv_sem=recv_sem.at[i, src],
             device_id={axis: src}, device_id_type=pl.DeviceIdType.MESH).wait_recv()
+
+    y_set = (y_send, y_recv)
+    u_set = (u_send, u_recv)
+    r_set = (r_send, r_recv)
 
     def noisy(k):
         c = jnp.full((1, tok_rows), sig_ref[k], F32)
@@ -183,13 +193,10 @@
         for d in range(1, n_dim):
             lin = lin + r[d:d + 1] * win_s[d]
         acts_s[...] = lin + astok_s[k]
-
-    def pack(k, b, r):
-        y_s[r, me] = (gate_s[k, b, 0] * norm_cols(acts_s[...]) + gate_s[k, b, 1]).astype(BF16)
-
-    def send(r):
-        for copy in copies(r):
-            copy.start()
+        return r
+
+    def pack(k, b):
+        return (gate_s[k, b, 0] * norm_cols(acts_s[...]) + gate_s[k, b, 1]).astype(BF16)
 
     pin = pin_ref[...]
     pwin_s[:, :tile] = expand(pin[:, :c_pair])
@@ -300,14 +307,21 @@
         wup_ts[b] = jnp.transpose(wup_ref[b])
         wdown_ts[b] = jnp.transpose(wdown_ref[b])
     z_copies[0].wait()
-    condition(0)
+    condition()
+    gates(0, 1)
     xs_s[...] = sig_ref[0] * x_ref[...]
     begin(0)
     for it in range(depth):
         trip(it)
-    pack(0, 0, 0)
+    y_s[0, me] = pack(0, 0)
+    for k in range(1, n_steps):
+        u_s[k, me] = u_own[k]
     pl.semaphore_wait(barrier, n_peers - 1)
-    send(0)
+    for copy in copies(y_s, 0, *y_set):
+        copy.start()
+    for k in range(1, n_steps):
+        for copy in copies(u_s, k, *u_set):
+            copy.start()
     z_copies[1].wait()
     lax.fori_loop(0, loops, trips, 0)
     for it in range(depth + loops * UNROLL, total + depth):
@@ -325,23 +339,38 @@
     chip_keys = cores * tok_rows
     my_chip = me // cores
 
+    def others(d, chip):
+        return [me + 1 - 2 * lax.rem(me, cores)] if d == 0 else [chip * cores + c for c in range(cores)]
+
     def block(k, b):
         r = k * n_blocks + b
-        y = y_s[r, me]
+        rebuilt = k > 0 and b == 0
+        y = pack(k, b) if rebuilt else y_s[r, me]
         q = dot(wqkvg_ts[b, :c_token, :], y)
         g = sigmoid(dot(wqkvg_ts[b, 3 * c_token:, :], y))
         q_heads = jnp.concatenate([jnp.where(head == h, q, 0.0).astype(BF16) for h in range(n_heads)], axis=1)
         tops, sums = [], []
         pos = 0
-        for group in GROUPS:
+        for group in GROUPS if r > 0 else (sum(GROUPS, ()),):
             chips = [lax.rem(my_chip + d, n_chips) for d in group]
             for d, chip in zip(group, chips):
-                if d == 0:
-                    wait_from(r, me + 1 - 2 * lax.rem(me, cores))
-                else:
-                    for c in range(cores):
-                        wait_from(r, chip * cores + c)
-            y_group = jnp.concatenate([y_s[r, chip * cores + c] for chip in chips for c in range(cores)], axis=1)
+                for src in others(d, chip):
+                    if rebuilt:
+                        wait_from(r_s, k, *r_set, src)
+                    else:
+                        wait_from(y_s, r, *y_set, src)
+            if rebuilt:
+                parts = []
+                for chip in chips:
+                    keys = pl.ds(pl.multiple_of(chip * chip_keys, chip_keys), chip_keys)
+                    pos_r = jnp.concatenate([r_s[k, chip * cores + c] for c in range(cores)], axis=1)
+                    lin = pos_r[0:1] * jnp.concatenate([win_s[0]] * cores, axis=1)
+                    for d in range(1, n_dim):
+                        lin = lin + pos_r[d:d + 1] * jnp.concatenate([win_s[d]] * cores, axis=1)
+                    parts.append((mul_all[:, keys] * norm_cols(lin + ast_all[:, keys]) + add_all[:, keys]).astype(BF16))
+                y_group = jnp.concatenate(parts, axis=1)
+            else:
+                y_group = jnp.concatenate([y_s[r, chip * cores + c] for chip in chips for c in range(cores)], axis=1)
             kv = dot(wqkvg_ts[b, c_token:3 * c_token, :], y_group).astype(BF16)
             vt_s[:, pos * chip_keys:(pos + len(group)) * chip_keys] = kv[c_token:]
             scores = dot_tn(kv[:c_token], q_heads)
@@ -371,38 +400,41 @@
         half = h.shape[0] // 2
         act = (silu(h[:half]) * h[half:]).astype(BF16)
         acts_s[...] = acts + gate_s[k, b, 5] * dot(wdown_ts[b], act)
-        for copy in copies(r):
+        for copy in copies(r_s, k, *r_set) if rebuilt else copies(y_s, r, *y_set):
             copy.wait_send()
 
     turn(0)
-
-    def step(k, carry):
-        @pl.when(k > 0)
-        def _():
-            begin(k)
-            pack(k, 0, k * n_blocks)
-            send(k * n_blocks)
-
+    r_s[...] = jnp.zeros(r_s.shape, F32)
+    for k in range(n_steps):
+        if k > 0:
+            r_s[k, me, :n_dim] = begin(k)
+            for copy in copies(r_s, k, *r_set):
+                copy.start()
+            for off in range(1, n_peers):
+                wait_from(u_s, k, *u_set, lax.rem(me + off, n_peers))
+            u_all = jnp.concatenate([u_s[k, src] for src in range(n_peers)], axis=1)
+            ast_all[...] = dot_tn(wstok_ref[...], u_all)
+            mul_all[...] = sigmoid(dot_tn(wcond_ref[0, :, :c_token], u_all))
+            add_all[...] = dot_tn(wcond_ref[0, :, c_token:2 * c_token], u_all)
         block(k, 0)
         for b in range(1, n_blocks):
-            pack(k, b, k * n_blocks + b)
-            send(k * n_blocks + b)
-
-            @pl.when(k == 0)
-            def _():
+            r = k * n_blocks + b
+            y_s[r, me] = pack(k, b)
+            for copy in copies(y_s, r, *y_set):
+                copy.start()
+            if k == 0:
                 turn(b)
-                if b == 1:
-                    for later in range(1, n_steps):
-                        condition(later)
-
+                if b == 1 and n_steps > 1:
+                    gates(1, n_steps)
             block(k, b)
+        if k == 0:
+            for later in range(1, n_steps):
+                for copy in copies(u_s, later, *u_set):
+                    copy.wait_send()
         xn, t, var = noisy(k)
         update = dot(wout_ref[...], norm_cols(acts_s[...]).astype(BF16))
         denoised = (SIGMA_DATA * SIGMA_DATA / var) * xn + (t * SIGMA_DATA / jnp.sqrt(var)) * update
         xs_s[...] = xn + STEP_SCALE * (sig_ref[k + 1] - t) * (xn - denoised) / t
-        return carry
-
-    lax.fori_loop(0, n_steps, step, 0)
     out_ref[...] = xs_s[...]
 
 
@@ -463,9 +495,19 @@
                 pltpu.VMEM((c_token, tok_rows), F32),
                 pltpu.VMEM((n_dim, tok_rows), F32),
                 pltpu.VMEM((n_rounds, n_peers, c_token, tok_rows), BF16),
+                pltpu.VMEM((n_steps, c_token, tok_rows), BF16),
+                pltpu.VMEM((n_steps, n_peers, c_token, tok_rows), BF16),
+                pltpu.VMEM((n_steps, n_peers, SUB, tok_rows), F32),
+                pltpu.VMEM((c_token, n_tok), F32),
+                pltpu.VMEM((c_token, n_tok), F32),
+                pltpu.VMEM((c_token, n_tok), F32),
                 pltpu.SemaphoreType.DMA((2,)),
                 pltpu.SemaphoreType.DMA((n_rounds, n_peers)),
                 pltpu.SemaphoreType.DMA((n_rounds, n_peers)),
+                pltpu.SemaphoreType.DMA((n_steps, n_peers)),
+                pltpu.SemaphoreType.DMA((n_steps, n_peers)),
+                pltpu.SemaphoreType.DMA((n_steps, n_peers)),
+                pltpu.SemaphoreType.DMA((n_steps, n_peers)),
             ],
             compiler_params=pltpu.CompilerParams(collective_id=0, has_side_effects=True, vmem_limit_bytes=60 * 1024 * 1024),
             name="sampler",

time: 70.8 us -> 69.3 us (0.979)
  Pallas kernels: 69.4 us -> 67.9 us
    pallas_call x1, Pallas kernels: 69.4 us -> 67.9 us  [local_run(): pl.pallas_call(functools.partial(kernel, 'tok', n_peers), in_specs=specs,...]
where the time goes in v5:
time: 69.3 us; the launch traced here: 69.2 us
  Pallas kernels  67.9 us (98%)
  local copies, waits for them, and re-layouts  1.26 us (2%)
    pallas_call x1, Pallas kernels, local_run(): pl.pallas_call(functools.partial(kernel, 'tok', n_peers), in_specs=specs,...  67.9 us

profile of v5, /device:TPU:112, one launch (start us, length us, event | category | flops | bytes accessed | tf_op | source)
XLA Modules:
  0.0 69.2 jit_solution(11797038956302874280)
XLA Ops:
  0.0 67.9 %sampler.1 = f32[3,128]{1,0:T(4,128)} custom-call(f32[4]{0:T(128)} %sig_ref.1, bf16[128,16,1024]{2,1,0:T(8,128)(2,1)} %bitcast.11, bf16[16,65]{1,0:T(8,128)(2,1)} %bitcast.15, bf16[16,32]{1,0:T(8,128)(2,1)} %bitcast.16, bf16[2,16,64]{2,1,0:T(8,128)(2,1)} %zup_ref.1, bf16[2,16,32]{2,1,0:T(8,128)(2,1)} %bitcast.13, bf16[2,4,16]{2,1,0:T(4,128)(2,1)} %bitcast.17, ...), custom_call_target="tpu_custom_call" | custom-call | tf_op jit(solution)/shard_map/sampler/pallas_call | solution.py:462
  67.9 1.3 %copy.28 = f32[128,3]{0,1:T(4,128)} copy(f32[128,3]{0,1:T(4,128)} %bitcast.12) | data formatting | bytes 3072

commit v6 on v5

--- a/solution.py
+++ b/solution.py
@@ -18,6 +18,8 @@
 SUB = 8
 CHUNK = 256
 UNROLL = 7
+PACE = 4
+SKEW = 2
 GROUPS = ((0,), (2, 1, 3))
 F32 = jnp.float32
 BF16 = jnp.bfloat16
@@ -81,6 +83,15 @@
 def silu(h):
     half = 0.5 * h
     return half + half * jnp.tanh(half)
+
+
+def weave(*parts):
+    parts = list(parts)
+    while parts:
+        for part in list(parts):
+            work, count = part
+            if any(next(work, part) is part for _ in range(count)):
+                parts.remove(part)
 
 
 def kernel(
@@ -92,7 +103,7 @@
     z_s, bias_s, pwin_s, pwup_s, pwdown_s, pwpb_s, perm_s, rel_s, relsum_s,
     zn_s, xn_ss, cond_ss, held_ss, act_ss,
     bias_ts, wqkvg_ts, wao_ts, wup_ts, wdown_ts, cols_s, win_s, e_s, vt_s,
-    base_s, four_s, astok_s, gate_s, acts_s, xs_s, y_s, u_own, u_s, r_s, ast_all, mul_all, add_all,
+    base_s, four_s, astok_s, gate_s, acts_s, xs_s, y_s, y_own, u_own, u_s, r_s, ast_all, mul_all, add_all,
     z_sem, y_send, y_recv, u_send, u_recv, r_send, r_recv,
 ):
     me = lax.axis_index(axis)
@@ -118,42 +129,54 @@
     for off in range(1, n_peers):
         pl.semaphore_signal(barrier, inc=1, device_id={axis: lax.rem(me + off, n_peers)}, device_id_type=pl.DeviceIdType.MESH)
 
-    row = lax.broadcasted_iota(jnp.int32, (SUB, 1), 0)
-    t_col = jnp.full((SUB, 1), sig_ref[0] * (1.0 + GAMMA), F32)
-    for k in range(1, n_steps):
-        t_col = jnp.where(row == k, sig_ref[k] * (1.0 + GAMMA), t_col)
-    level = 0.25 * jnp.log(t_col / SIGMA_DATA)
-    feat = jnp.cos(2.0 * math.pi * (level * fw_ref[...] + fb_ref[...]))
-    four_s[...] = lax.dot_general(wfour_ref[...], norm_rows(feat).astype(BF16), (((0,), (1,)), ((), ())), preferred_element_type=F32)
-    joined = norm_rows(jnp.concatenate([st_ref[...].astype(F32), si_ref[...].astype(F32)], axis=-1)).astype(BF16)
-    base_s[...] = lax.dot_general(wsingle_ref[...], joined, (((0,), (1,)), ((), ())), preferred_element_type=F32)
     n_dim = x_ref.shape[0]
-    small = [gbias_ref[b] for b in range(n_blocks)] + [win_ref[...]]
-    n_small = 2 * n_blocks + n_dim
-    cols = jnp.transpose(jnp.concatenate(small + [jnp.zeros((-n_small % SUB, c_token), F32)], axis=0))
-    cols_s[...] = cols
-    for d in range(n_dim):
-        win_s[d] = jnp.broadcast_to(cols[:, 2 * n_blocks + d:2 * n_blocks + d + 1], (c_token, tok_rows))
+
+    def prepare():
+        row = lax.broadcasted_iota(jnp.int32, (SUB, 1), 0)
+        t_col = jnp.full((SUB, 1), sig_ref[0] * (1.0 + GAMMA), F32)
+        for k in range(1, n_steps):
+            t_col = jnp.where(row == k, sig_ref[k] * (1.0 + GAMMA), t_col)
+        level = 0.25 * jnp.log(t_col / SIGMA_DATA)
+        feat = jnp.cos(2.0 * math.pi * (level * fw_ref[...] + fb_ref[...]))
+        yield
+        four_s[...] = lax.dot_general(wfour_ref[...], norm_rows(feat).astype(BF16), (((0,), (1,)), ((), ())), preferred_element_type=F32)
+        yield
+        joined = norm_rows(jnp.concatenate([st_ref[...].astype(F32), si_ref[...].astype(F32)], axis=-1)).astype(BF16)
+        base_s[...] = lax.dot_general(wsingle_ref[...], joined, (((0,), (1,)), ((), ())), preferred_element_type=F32)
+        yield
+        small = [gbias_ref[b] for b in range(n_blocks)] + [win_ref[...]]
+        n_small = 2 * n_blocks + n_dim
+        cols = jnp.transpose(jnp.concatenate(small + [jnp.zeros((-n_small % SUB, c_token), F32)], axis=0))
+        cols_s[...] = cols
+        for d in range(n_dim):
+            win_s[d] = jnp.broadcast_to(cols[:, 2 * n_blocks + d:2 * n_blocks + d + 1], (c_token, tok_rows))
+        yield
+        yield from condition()
 
     def condition():
         single = jnp.concatenate([base_s[...] + four_s[:, k:k + 1] for k in range(n_steps)], axis=1)
         for layer in range(wsup_ref.shape[0]):
             h = dot_tn(wsup_ref[layer], norm_cols(single).astype(BF16))
+            yield
             half = h.shape[0] // 2
             act = (silu(h[:half]) * h[half:]).astype(BF16)
             single = single + dot_tn(wsdown_ref[layer], act)
+            yield
         u = norm_cols(single).astype(BF16)
         for k in range(n_steps):
             u_own[k] = u[:, k * tok_rows:(k + 1) * tok_rows]
+        yield
 
     def gates(first, last):
         u = jnp.concatenate([u_own[k] for k in range(first, last)], axis=1)
         acts = dot_tn(wstok_ref[...], u)
+        yield
         at = lambda v, k: v[:, (k - first) * tok_rows:(k - first + 1) * tok_rows]
         for k in range(first, last):
             astok_s[k] = at(acts, k)
         for b in range(n_blocks):
             cond = dot_tn(wcond_ref[b], u)
+            yield
             part = lambda i: cond[i * c_token:(i + 1) * c_token]
             rows = [sigmoid(part(0)), part(1), sigmoid(part(2) + cols_s[:, 2 * b:2 * b + 1]), sigmoid(part(3)), part(4), sigmoid(part(5) + cols_s[:, 2 * b + 1:2 * b + 2])]
             for i, gate in enumerate(rows):
@@ -198,45 +221,54 @@
     def pack(k, b):
         return (gate_s[k, b, 0] * norm_cols(acts_s[...]) + gate_s[k, b, 1]).astype(BF16)
 
-    pin = pin_ref[...]
-    pwin_s[:, :tile] = expand(pin[:, :c_pair])
-    pwin_s[:, tile:] = expand(pin[:, c_pair:])
-    for layer in range(n_layers):
-        up = zup_ref[layer]
-        width = up.shape[1]
-        full = expand_tall(dot_t(spread(width), up))
-        gate_rows = lax.broadcasted_iota(jnp.int32, full.shape, 0) < (width // 2) * SUB
-        pwup_s[layer] = jnp.where(gate_rows, 0.5 * full, full).astype(BF16)
-        pwdown_s[layer] = expand(zdown_ref[layer])
-    for b in range(n_blocks):
-        pwpb_s[b * n_heads * SUB:(b + 1) * n_heads * SUB, :] = expand(pb_ref[b])
-    rows_i = lax.broadcasted_iota(jnp.int32, (tile, tile), 0)
-    cols_i = lax.broadcasted_iota(jnp.int32, (tile, tile), 1)
-    perm_s[...] = ((rows_i & (SUB - 1)) * c_pair + rows_i // SUB == cols_i).astype(BF16)
-    tall = dot(spread(c_pair), rel_ref[...]).astype(BF16)
-    bin_i = lax.broadcasted_iota(jnp.int32, (n_bins, LANES), 0)
-    diag_i = lax.broadcasted_iota(jnp.int32, (n_bins, LANES), 1)
-    row_s = lax.broadcasted_iota(jnp.int32, (tile, LANES), 0) & (SUB - 1)
-    tab = jnp.zeros((tile, LANES), F32)
-    for s in range(SUB):
-        pick = (bin_i == jnp.clip(diag_i - (SUB - 1) + s, 0, n_bins - 1)).astype(BF16)
-        tab = jnp.where(row_s == s, dot(tall, pick), tab)
-    tab = tab.astype(BF16)
-
-    per = 2
-    k_i = lax.broadcasted_iota(jnp.int32, (LANES, LANES), 0)
-    j_i = lax.broadcasted_iota(jnp.int32, (LANES, LANES), 1)
-
-    for i in range(0, n_var, per):
-        picks = []
-        for v in range(i, i + per):
-            want = jnp.clip(SUB * (v - low) - j_i + clip + SUB - 1, 0, n_bins + SUB - 2)
-            picks.append((k_i == want).astype(BF16))
-        planes = dot(tab, jnp.concatenate(picks, axis=1))
-        for v in range(i, i + per):
-            plane = planes[:, (v - i) * LANES:(v - i + 1) * LANES]
-            rel_s[v] = plane
-            relsum_s[v] = jnp.sum(plane.reshape(c_pair, SUB, LANES), axis=0)
+    def tables():
+        pin = pin_ref[...]
+        pwin_s[:, :tile] = expand(pin[:, :c_pair])
+        yield
+        pwin_s[:, tile:] = expand(pin[:, c_pair:])
+        yield
+        for layer in range(n_layers):
+            up = zup_ref[layer]
+            width = up.shape[1]
+            full = expand_tall(dot_t(spread(width), up))
+            gate_rows = lax.broadcasted_iota(jnp.int32, full.shape, 0) < (width // 2) * SUB
+            pwup_s[layer] = jnp.where(gate_rows, 0.5 * full, full).astype(BF16)
+            yield
+            pwdown_s[layer] = expand(zdown_ref[layer])
+            yield
+        for b in range(n_blocks):
+            pwpb_s[b * n_heads * SUB:(b + 1) * n_heads * SUB, :] = expand(pb_ref[b])
+            yield
+        rows_i = lax.broadcasted_iota(jnp.int32, (tile, tile), 0)
+        cols_i = lax.broadcasted_iota(jnp.int32, (tile, tile), 1)
+        perm_s[...] = ((rows_i & (SUB - 1)) * c_pair + rows_i // SUB == cols_i).astype(BF16)
+        yield
+        tall = dot(spread(c_pair), rel_ref[...]).astype(BF16)
+        bin_i = lax.broadcasted_iota(jnp.int32, (n_bins, LANES), 0)
+        diag_i = lax.broadcasted_iota(jnp.int32, (n_bins, LANES), 1)
+        row_s = lax.broadcasted_iota(jnp.int32, (tile, LANES), 0) & (SUB - 1)
+        tab = jnp.zeros((tile, LANES), F32)
+        for s in range(SUB):
+            pick = (bin_i == jnp.clip(diag_i - (SUB - 1) + s, 0, n_bins - 1)).astype(BF16)
+            tab = jnp.where(row_s == s, dot(tall, pick), tab)
+            yield
+        tab = tab.astype(BF16)
+
+        per = 2
+        k_i = lax.broadcasted_iota(jnp.int32, (LANES, LANES), 0)
+        j_i = lax.broadcasted_iota(jnp.int32, (LANES, LANES), 1)
+
+        for i in range(0, n_var, per):
+            picks = []
+            for v in range(i, i + per):
+                want = jnp.clip(SUB * (v - low) - j_i + clip + SUB - 1, 0, n_bins + SUB - 2)
+                picks.append((k_i == want).astype(BF16))
+            planes = dot(tab, jnp.concatenate(picks, axis=1))
+            yield
+            for v in range(i, i + per):
+                plane = planes[:, (v - i) * LANES:(v - i + 1) * LANES]
+                rel_s[v] = plane
+                relsum_s[v] = jnp.sum(plane.reshape(c_pair, SUB, LANES), axis=0)
 
     n_chunks = n_tok // CHUNK
     total = (tok_rows // SUB) * n_chunks
@@ -253,31 +285,33 @@
             r0, c0 = (idx // n_chunks) * SUB, (idx % n_chunks) * CHUNK
             return (r0, c0) if known else (pl.multiple_of(r0, SUB), pl.multiple_of(c0, CHUNK))
 
-        if active(depth):
+        def out_store(bias):
             r0, c0 = place(depth)
-            bias = dot(pwpb_s[...], xn_ss[n_layers])
             bias = bias.astype(BF16).astype(F32) * LOG2E
             bias_s[:, pl.ds(r0, SUB), pl.ds(c0, CHUNK)] = bias.reshape(n_blocks * n_heads, SUB, CHUNK)
-        for layer in reversed(range(n_layers)):
-            if active(3 + 2 * layer):
-                cond = held_ss[layer] + dot(pwdown_s[layer], act_ss[layer])
-                xn_ss[layer + 1] = norm_major(cond)
-            if active(2 + 2 * layer):
-                h = dot(pwup_s[layer], xn_ss[layer])
-                half = h.shape[0] // 2
-                gate = h[:half]
-                act_ss[layer] = ((gate + gate * jnp.tanh(gate)) * h[half:]).astype(BF16)
-                held_ss[layer] = cond_ss[layer]
-            if active(3 + 2 * layer) and layer + 1 < n_layers:
+
+        def down_store(layer, cond):
+            xn_ss[layer + 1] = norm_major(cond)
+            if layer + 1 < n_layers:
                 cond_ss[layer + 1] = cond
-        if active(1):
-            cond = dot(pwin_s[...], zn_s[...])
+
+        def up_store(layer, h):
+            half = h.shape[0] // 2
+            gate = h[:half]
+            act_ss[layer] = ((gate + gate * jnp.tanh(gate)) * h[half:]).astype(BF16)
+            held_ss[layer] = cond_ss[layer]
+
+        def in_store(cond):
             cond_ss[0] = cond
             xn_ss[0] = norm_major(cond)
-        if active(0):
+
+        def turn_rows():
             r0, c0 = place(0)
             zb = z_s[pl.ds(r0, SUB), :, pl.ds(c0, CHUNK)].reshape(tile, CHUNK)
-            z = dot(perm_s[...], zb).reshape(c_pair, SUB, CHUNK)
+            return dot(perm_s[...], zb).reshape(c_pair, SUB, CHUNK)
+
+        def pair_store(z):
+            r0, c0 = place(0)
             rels, sums = [], []
             for part in range(CHUNK // LANES):
                 delta = me * tok_rows + r0 - c0 - part * LANES
@@ -294,26 +328,58 @@
             zn_s[:tile] = (zc * rs).reshape(tile, CHUNK).astype(BF16)
             zn_s[tile:] = (rc * rs).reshape(tile, CHUNK).astype(BF16)
 
+        stages = []
+        if active(depth):
+            stages.append((lambda: dot(pwpb_s[...], xn_ss[n_layers]), out_store))
+        for layer in reversed(range(n_layers)):
+            if active(3 + 2 * layer):
+                stages.append((lambda layer=layer: held_ss[layer] + dot(pwdown_s[layer], act_ss[layer]), functools.partial(down_store, layer)))
+            if active(2 + 2 * layer):
+                stages.append((lambda layer=layer: dot(pwup_s[layer], xn_ss[layer]), functools.partial(up_store, layer)))
+        if active(1):
+            stages.append((lambda: dot(pwin_s[...], zn_s[...]), in_store))
+        if active(0):
+            stages.append((turn_rows, pair_store))
+        return stages
+
+    def run(its):
+        waiting = []
+        for it in its:
+            stages = trip(it)
+            for first_half, second_half in stages:
+                waiting.append(functools.partial(second_half, first_half()))
+                if len(waiting) > SKEW:
+                    waiting.pop(0)()
+            while waiting and len(stages) < SKEW + 2:
+                waiting.pop(0)()
+            yield
+        for rest in waiting:
+            rest()
+
     loops = (total - depth) // UNROLL
 
     def trips(i, carry):
-        for j in range(UNROLL):
-            trip(depth + i * UNROLL + j)
+        weave((run([depth + i * UNROLL + j for j in range(UNROLL)]), 1))
         return carry
 
-    for b in range(n_blocks):
-        wqkvg_ts[b] = jnp.transpose(wqkvg_ref[b])
-        wao_ts[b] = jnp.transpose(wao_ref[b])
-        wup_ts[b] = jnp.transpose(wup_ref[b])
-        wdown_ts[b] = jnp.transpose(wdown_ref[b])
+    def turned():
+        for b in range(n_blocks):
+            for src, dst in ((wqkvg_ref, wqkvg_ts), (wao_ref, wao_ts), (wup_ref, wup_ts), (wdown_ref, wdown_ts)):
+                dst[b] = jnp.transpose(src[b])
+                yield
+
+    weave((prepare(), 1), (tables(), PACE), (turned(), 1))
     z_copies[0].wait()
-    condition()
-    gates(0, 1)
-    xs_s[...] = sig_ref[0] * x_ref[...]
-    begin(0)
-    for it in range(depth):
-        trip(it)
-    y_s[0, me] = pack(0, 0)
+
+    def start():
+        yield from gates(0, 1)
+        xs_s[...] = sig_ref[0] * x_ref[...]
+        begin(0)
+        yield
+        y_own[...] = pack(0, 0)
+
+    weave((start(), 1), (run(range(depth)), 1))
+    y_s[0, me] = y_own[...]
     for k in range(1, n_steps):
         u_s[k, me] = u_own[k]
     pl.semaphore_wait(barrier, n_peers - 1)
@@ -324,8 +390,7 @@
             copy.start()
     z_copies[1].wait()
     lax.fori_loop(0, loops, trips, 0)
-    for it in range(depth + loops * UNROLL, total + depth):
-        trip(it)
+    weave((run(range(depth + loops * UNROLL, total + depth)), 1))
 
     def turn(b):
         for h in range(n_heads):
@@ -425,7 +490,7 @@
             if k == 0:
                 turn(b)
                 if b == 1 and n_steps > 1:
-                    gates(1, n_steps)
+                    weave((gates(1, n_steps), 1))
             block(k, b)
         if k == 0:
             for later in range(1, n_steps):
@@ -495,6 +560,7 @@
                 pltpu.VMEM((c_token, tok_rows), F32),
                 pltpu.VMEM((n_dim, tok_rows), F32),
                 pltpu.VMEM((n_rounds, n_peers, c_token, tok_rows), BF16),
+                pltpu.VMEM((c_token, tok_rows), BF16),
                 pltpu.VMEM((n_steps, c_token, tok_rows), BF16),
                 pltpu.VMEM((n_steps, n_peers, c_token, tok_rows), BF16),
                 pltpu.VMEM((n_steps, n_peers, SUB, tok_rows), F32),

time: 69.3 us -> 68.6 us (0.990)
  Pallas kernels: 67.9 us -> 67.2 us
where the time goes in v6:
time: 68.6 us; the launch traced here: 68.5 us
  Pallas kernels  67.2 us (98%)
  local copies, waits for them, and re-layouts  1.26 us (2%)
    pallas_call x1, Pallas kernels, local_run(): pl.pallas_call(functools.partial(kernel, 'tok', n_peers), in_specs=specs,...  67.2 us

profile of v6, /device:TPU:112, one launch (start us, length us, event | category | flops | bytes accessed | tf_op | source)
XLA Modules:
  0.0 68.5 jit_solution(17400080871432247072)
XLA Ops:
  0.0 67.2 %sampler.1 = f32[3,128]{1,0:T(4,128)} custom-call(f32[4]{0:T(128)} %sig_ref.1, bf16[128,16,1024]{2,1,0:T(8,128)(2,1)} %bitcast.11, bf16[16,65]{1,0:T(8,128)(2,1)} %bitcast.15, bf16[16,32]{1,0:T(8,128)(2,1)} %bitcast.16, bf16[2,16,64]{2,1,0:T(8,128)(2,1)} %zup_ref.1, bf16[2,16,32]{2,1,0:T(8,128)(2,1)} %bitcast.13, bf16[2,4,16]{2,1,0:T(4,128)(2,1)} %bitcast.17, ...), custom_call_target="tpu_custom_call" | custom-call | tf_op jit(solution)/shard_map/sampler/pallas_call | solution.py:527
  67.2 1.3 %copy.28 = f32[128,3]{0,1:T(4,128)} copy(f32[128,3]{0,1:T(4,128)} %bitcast.12) | data formatting | bytes 3072

commit v7 on v6

--- a/solution.py
+++ b/solution.py
@@ -16,8 +16,8 @@
 LOG2E = math.log2(math.e)
 LANES = 128
 SUB = 8
-CHUNK = 256
-UNROLL = 7
+CHUNK = 512
+UNROLL = 4
 PACE = 4
 SKEW = 2
 GROUPS = ((0,), (2, 1, 3))

time: 68.6 us -> 68.3 us (level)
  no operation moved by 1% of the time
where the time goes in v7:
time: 68.3 us; the launch traced here: 68.2 us
  Pallas kernels  66.9 us (98%)
  local copies, waits for them, and re-layouts  1.26 us (2%)
    pallas_call x1, Pallas kernels, local_run(): pl.pallas_call(functools.partial(kernel, 'tok', n_peers), in_specs=specs,...  66.9 us

profile of v7, /device:TPU:112, one launch (start us, length us, event | category | flops | bytes accessed | tf_op | source)
XLA Modules:
  0.0 68.2 jit_solution(3345514749393194826)
XLA Ops:
  0.0 66.9 %sampler.1 = f32[3,128]{1,0:T(4,128)} custom-call(f32[4]{0:T(128)} %sig_ref.1, bf16[128,16,1024]{2,1,0:T(8,128)(2,1)} %bitcast.11, bf16[16,65]{1,0:T(8,128)(2,1)} %bitcast.15, bf16[16,32]{1,0:T(8,128)(2,1)} %bitcast.16, bf16[2,16,64]{2,1,0:T(8,128)(2,1)} %zup_ref.1, bf16[2,16,32]{2,1,0:T(8,128)(2,1)} %bitcast.13, bf16[2,4,16]{2,1,0:T(4,128)(2,1)} %bitcast.17, ...), custom_call_target="tpu_custom_call" | custom-call | tf_op jit(solution)/shard_map/sampler/pallas_call | solution.py:527
  66.9 1.3 %copy.28 = f32[128,3]{0,1:T(4,128)} copy(f32[128,3]{0,1:T(4,128)} %bitcast.12) | data formatting | bytes 3072
